TPU v7x, 8 devices: a whole 2x2x1 slice. The times are simulated.
8 devices in a mesh: pz: 2 (over z, y), py: 2 (over x), px: 2 (over core).
Axes of the slice: x: 2, y: 2, z: 1, core: 2. Of those that a mesh axis runs over, the one named last changes fastest.
Arguments:
- shift_diag: float32 [2, 128, 128, 128], P(None, 'px', 'py', 'pz')
- rhs_field: float32 [2, 128, 128, 128], P(None, 'px', 'py', 'pz')
- x_start: float32 [2, 128, 128, 128], P(None, 'px', 'py', 'pz')
- cond_x: float32 [2, 128, 128, 128], P(None, 'px', 'py', 'pz')
- cond_y: float32 [2, 128, 128, 128], P(None, 'px', 'py', 'pz')
- cond_z: float32 [2, 128, 128, 128], P(None, 'px', 'py', 'pz')
Outputs:
- output 1: float32 [2, 128, 128, 128], P(None, 'px', 'py', 'pz')
- output 2: float32 [2, 21], replicated
All inputs are finite; a program needn't handle non-finite values.
Results may differ from a plain program's by a relative error of at most 0.001.
Values sent between devices are 32-bit elements.
A program may use at most 1 GiB of HBM per device.

v0:
```python
import jax
import jax.numpy as jnp
from jax import lax
from jax.sharding import PartitionSpec as P

ITERS = 20
GRID_AXES = ('px', 'py', 'pz')
ALL_AXES = ('pz', 'py', 'px')


def up_pairs(axis_size):
    return [(dev_idx, dev_idx + 1) for dev_idx in range(axis_size - 1)]


def down_pairs(axis_size):
    return [(dev_idx, dev_idx - 1) for dev_idx in range(1, axis_size)]


def neighbour_planes(field, axis_name, axis_dim, axis_size):
    planes = field.shape[axis_dim]
    first_plane = lax.slice_in_dim(field, 0, 1, axis=axis_dim)
    last_plane = lax.slice_in_dim(field, planes - 1, planes, axis=axis_dim)
    from_below = lax.ppermute(last_plane, axis_name, up_pairs(axis_size))
    from_above = lax.ppermute(first_plane, axis_name, down_pairs(axis_size))
    return from_below, from_above


def extend_conduct(conduct, axis_name, axis_dim, axis_size):
    planes = conduct.shape[axis_dim]
    plane_index = lax.broadcasted_iota(jnp.int32, tuple(planes if pos_dim == axis_dim else 1 for pos_dim in range(conduct.ndim)), axis_dim)
    at_edge = jnp.logical_and(lax.axis_index(axis_name) == axis_size - 1, plane_index == planes - 1)
    masked = jnp.where(at_edge, 0.0, conduct)
    lower_faces = lax.ppermute(lax.slice_in_dim(conduct, planes - 1, planes, axis=axis_dim), axis_name, up_pairs(axis_size))
    return jnp.concatenate([lower_faces, masked], axis=axis_dim)


def apply_local(field, shift_diag, cond_ext, axis_sizes):
    halo_pairs = [neighbour_planes(field, GRID_AXES[axis_pos], axis_pos + 1, axis_sizes[axis_pos]) for axis_pos in range(3)]
    result = shift_diag * field
    for axis_pos in range(3):
        axis_dim = axis_pos + 1
        planes = field.shape[axis_dim]
        padded = jnp.concatenate([halo_pairs[axis_pos][0], field, halo_pairs[axis_pos][1]], axis=axis_dim)
        face_flux = cond_ext[axis_pos] * (lax.slice_in_dim(padded, 0, planes + 1, axis=axis_dim) - lax.slice_in_dim(padded, 1, planes + 2, axis=axis_dim))
        result = result + (lax.slice_in_dim(face_flux, 1, planes + 1, axis=axis_dim) - lax.slice_in_dim(face_flux, 0, planes, axis=axis_dim))
    return result


def solution(mesh):
    axis_sizes = tuple(mesh.shape[axis_name] for axis_name in GRID_AXES)
    field_spec = P(None, 'px', 'py', 'pz')

    def local_solve(shift_diag, rhs_field, x_start, cond_x, cond_y, cond_z):
        cell_count = x_start.shape[1] * x_start.shape[2] * x_start.shape[3] * axis_sizes[0] * axis_sizes[1] * axis_sizes[2]
        cond_ext = [extend_conduct(conduct, GRID_AXES[axis_pos], axis_pos + 1, axis_sizes[axis_pos]) for axis_pos, conduct in enumerate((cond_x, cond_y, cond_z))]

        def global_dot(left_vec, right_vec):
            return lax.psum(jnp.sum(left_vec * right_vec, axis=(1, 2, 3)), ALL_AXES)

        residual = rhs_field - apply_local(x_start, shift_diag, cond_ext, axis_sizes)
        rho_start = global_dot(residual, residual)

        def cg_step(loop_state, unused):
            x_cur, res_cur, direction, rho_old, beta_coef = loop_state
            direction = res_cur + beta_coef[:, None, None, None] * direction
            q_vec = apply_local(direction, shift_diag, cond_ext, axis_sizes)
            alpha_step = rho_old / global_dot(direction, q_vec)
            x_cur = x_cur + alpha_step[:, None, None, None] * direction
            res_cur = res_cur - alpha_step[:, None, None, None] * q_vec
            rho_new = global_dot(res_cur, res_cur)
            return (x_cur, res_cur, direction, rho_new, rho_new / rho_old), jnp.sqrt(rho_new / cell_count)

        init_state = (x_start, residual, jnp.zeros_like(residual), rho_start, jnp.zeros_like(rho_start))
        final_state, res_tail = lax.scan(cg_step, init_state, None, length=ITERS)
        res_hist = jnp.concatenate([jnp.sqrt(rho_start / cell_count)[None], res_tail], axis=0).T
        return final_state[0], res_hist

    return jax.shard_map(local_solve, mesh=mesh, in_specs=(field_spec, field_spec, field_spec, field_spec, field_spec, field_spec), out_specs=(field_spec, P(None, None)), check_vma=False)
```

profile of v0, /device:TPU:0, one launch (start us, length us, event | category | flops | bytes accessed | tf_op | source)
XLA Modules:
  0.0 2710.3 jit_solution(18180642209269302430)
XLA Ops:
  146.3 2556.3 %while.21 = (s32[]{:T(128)}, f32[2,64,64,64]{3,1,2,0:T(8,128)}, f32[2,64,64,64]{3,1,2,0:T(8,128)}, f32[2,64,64,64]{3,1,2,0:T(8,128)}, f32[2]{0:T(128)}, /*index=...) while((s32[]{:T(128)}, f32[2,64,64,64]{3,1,2,0:T(8,128)}, ...), condition=%wide.region_7.8_spmd.clone, body=%wide.region_2.7_spmd.clone.sunk | while | flops 15826955 | bytes 79889072 | solution.py:74
  210.6 25.4 psum.26
  247.6 23.0 psum.27
  338.5 25.4 psum.26
  375.5 23.0 psum.27
  466.4 25.4 psum.26
  503.4 23.0 psum.27
  594.4 25.4 psum.26
  722.3 25.4 psum.26
  759.3 23.0 psum.27
  850.2 25.4 psum.26
  887.2 23.0 psum.27
  978.1 25.4 psum.26
  1015.1 23.0 psum.27
  1106.0 25.4 psum.26
  1143.0 23.0 psum.27
  1233.9 25.4 psum.26
  1361.8 25.4 psum.26
  1398.8 23.0 psum.27
  1489.7 25.4 psum.26
  1617.7 25.4 psum.26
  1654.7 23.0 psum.27
  1745.6 25.4 psum.26
  1782.6 23.0 psum.27
  1873.5 25.4 psum.26
  1910.5 23.0 psum.27
  2001.4 25.4 psum.26
  2129.3 25.4 psum.26
  2257.2 25.4 psum.26
  2385.1 25.4 psum.26
  2513.0 25.4 psum.26
  2641.0 25.4 psum.26
  (900 shorter events, 1943.1 us)
Async XLA Ops:
  7.4 75.6 %collective-permute-start.10 = (f32[2,64,1,64]{3,1,2,0:T(8,128)S(1)}, f32[2,64,1,64]{3,1,2,0:T(8,128)S(1)}, u32[]{:S(2)}, u32[]{:S(2)}) collective-permute-start(f32[2,64,1,64]{3,1,2,0:T(8,128)S(1)} %get-tuple-element.171), channel_id=1, source_target_pairs={{0,2},{1,3},{4,6},{5,7}} | collective-permute-start | bytes 98312 | tf_op jit(solution)/shard_map/ppermute | solution.py:23
  12.6 73.8 %collective-permute-start.11 = (f32[2,64,1,64]{3,1,2,0:T(8,128)S(1)}, f32[2,64,1,64]{3,1,2,0:T(8,128)S(1)}, u32[]{:S(2)}, u32[]{:S(2)}) collective-permute-start(f32[2,64,1,64]{3,1,2,0:T(8,128)S(1)} %get-tuple-element.170), channel_id=1, source_target_pairs={{2,0},{3,1},{6,4},{7,5}} | collective-permute-start | bytes 98312 | tf_op jit(solution)/shard_map/ppermute | solution.py:24
  15.0 71.4 %collective-permute-start.9 = (f32[2,64,1,64]{3,1,2,0:T(8,128)S(1)}, f32[2,64,1,64]{3,1,2,0:T(8,128)S(1)}, u32[]{:S(2)}, u32[]{:S(2)}) collective-permute-start(f32[2,64,1,64]{3,1,2,0:T(8,128)S(1)} %copy.78), channel_id=1, source_target_pairs={{0,2},{1,3},{4,6},{5,7}} | collective-permute-start | bytes 98312 | tf_op jit(solution)/shard_map/ppermute | solution.py:33
  27.4 33.1 %collective-permute-start.13 = (f32[2,64,64,1]{2,1,3,0:T(8,128)S(1)}, f32[2,64,64,1]{2,1,3,0:T(8,128)S(1)}, u32[]{:S(2)}, u32[]{:S(2)}) collective-permute-start(f32[2,64,64,1]{2,1,3,0:T(8,128)S(1)} %copy.70), channel_id=1, source_target_pairs={{0,4},{1,5},{2,6},{3,7}} | collective-permute-start | bytes 98312 | tf_op jit(solution)/shard_map/ppermute | solution.py:23
  75.9 26.7 collective-permute-start.7
  178.1 25.1 collective-permute-start.2
  180.1 23.2 collective-permute-start.3
  304.6 26.5 collective-permute-start.2
  308.0 23.2 collective-permute-start.3
  432.5 26.5 collective-permute-start.2
  435.9 23.2 collective-permute-start.3
  560.4 26.5 collective-permute-start.2
  563.8 23.2 collective-permute-start.3
  688.3 26.5 collective-permute-start.2
  691.7 23.2 collective-permute-start.3
  816.2 26.5 collective-permute-start.2
  944.2 26.5 collective-permute-start.2
  1072.1 26.5 collective-permute-start.2
  1200.0 26.5 collective-permute-start.2
  1327.9 26.5 collective-permute-start.2
  1455.8 26.5 collective-permute-start.2
  1459.2 23.2 collective-permute-start.3
  1583.7 26.5 collective-permute-start.2
  1711.6 26.5 collective-permute-start.2
  1839.5 26.5 collective-permute-start.2
  1967.5 26.5 collective-permute-start.2
  2095.4 26.5 collective-permute-start.2
  2223.3 26.5 collective-permute-start.2
  2351.2 26.5 collective-permute-start.2
  2354.6 23.2 collective-permute-start.3
  2479.1 26.5 collective-permute-start.2
  2607.0 26.5 collective-permute-start.2
  (207 other events, 5097.2 us)
where the time goes:
time: 2720 us; the launch traced here: 2710 us
  blocking collectives  991 us (36%)
  other arithmetic  783 us (29%)
  local copies, waits for them, and re-layouts  650 us (24%)
  starting transfers between devices  280 us (10%)
    psum x41, blocking collectives, global_dot(): return lax.psum(jnp.sum(left_vec * right_vec, axis=(1, 2, 3)), ALL_AXES)  991 us
    reduce_sum x41, other arithmetic, global_dot(): return lax.psum(jnp.sum(left_vec * right_vec, axis=(1, 2, 3)), ALL_AXES)  359 us
    slice x83, local copies, waits for them, and re-layouts, neighbour_planes(): first_plane = lax.slice_in_dim(field, 0, 1, axis=axis_dim)  284 us
    mul x61, other arithmetic, apply_local(): cond_ext[axis_pos]  224 us
    ppermute x63, starting transfers between devices, neighbour_planes(): from_below = lax.ppermute(last_plane, axis_name, up_pairs(axis_size))  186 us
    add x20, other arithmetic, cg_step(): direction = res_cur + beta_coef[:, None, None, None] * direction  138 us
    ppermute x21, local copies, waits for them, and re-layouts, neighbour_planes(): from_below = lax.ppermute(last_plane, axis_name, up_pairs(axis_size))  96.1 us
    ppermute x21, local copies, waits for them, and re-layouts, neighbour_planes(): from_above = lax.ppermute(first_plane, axis_name, down_pairs(axis_size))  93.4 us
  transfers between devices with their start and end apart: 129, of which 0 were waited for; matrix products, arithmetic and copies ran while one was open for 21% of the time, Pallas kernels for 0%

commit v1 on v0

v1 whole, which is shorter than its diff:
```python
import jax
import jax.numpy as jnp
from jax import lax
from jax.experimental import pallas as pl
from jax.experimental.pallas import tpu as pltpu
from jax.sharding import PartitionSpec as P

ITERS = 20
F32 = jnp.float32
MESH = pl.DeviceIdType.MESH

NP = 32
NR = 64
LN = 128
PR = 80
KR = 72
SYS = NP * NR
PSYS = (NP + 1) * PR
KSYS = NP * KR


def roll(val, shift):
    if isinstance(shift, int):
        shift = shift % LN
    return pltpu.roll(val, shift, 1)


def kernel(s_hbm, b_hbm, x0_hbm, kx_hbm, ky_hbm, kz_hbm, x_out, hist_out,
           st_s, st_b, st_x, st_kx, st_ky, st_kz,
           R, Q, PB, KX, KXM, KY, KZ, D, KF,
           ix, iy, iz, jx, jy, jz, sxy, sxz, sky, skz, sy, sz,
           rhx, rhy, rhz, phx, phy, phz, qhx, qhy, qhz,
           red, rho_s, alpha_s, hist_s,
           ld_sem, isend, irecv, rsend, rrecv, qsend, qrecv, dsend, drecv):
    X = x_out
    pz, py, px = lax.axis_index('pz'), lax.axis_index('py'), lax.axis_index('px')
    nbr = {'x': (pz, py, 1 - px), 'y': (pz, 1 - py, px), 'z': (1 - pz, py, px)}
    others = {}
    for m in range(1, 8):
        others[m] = (1 - pz if m & 4 else pz, 1 - py if m & 2 else py, 1 - px if m & 1 else px)

    lane = lax.broadcasted_iota(jnp.int32, (8, LN), 1)
    row8 = lax.broadcasted_iota(jnp.int32, (8, LN), 0)

    def lanes(n):
        return lax.broadcasted_iota(jnp.int32, (n, LN), 1)

    zf = 63 * (1 - pz)
    xf = 31 * (1 - px)
    yf = 63 * (1 - py)
    hrow = 72 - 65 * py
    to_z = 127 - 126 * pz
    fro_z = 1 + 126 * pz

    def face_mask(n):
        return (lanes(n) % 64) == zf

    def splits(n):
        return lanes(n) < 64

    loads = []
    for num, (src, dst) in enumerate(((x0_hbm, st_x), (kz_hbm, st_kz), (kx_hbm, st_kx), (ky_hbm, st_ky), (s_hbm, st_s), (b_hbm, st_b))):
        pair = [pltpu.make_async_copy(src.at[c], dst.at[c], ld_sem.at[num, c]) for c in range(2)]
        for cp in pair:
            cp.start()
        loads.append(pair)

    barrier = pltpu.get_barrier_semaphore()
    for m in range(1, 8):
        pl.semaphore_signal(barrier, inc=1, device_id=others[m], device_id_type=MESH)

    def packed(st, c, x):
        return jnp.concatenate([st[c, x], st[c, x + NP]], axis=1)

    def pick(T, val, x, f):
        l64 = lanes(32) % 64
        T = jnp.where(l64 == x, roll(val[:32], (x - f + LN) % LN), T)
        return jnp.where(l64 == x + 32, roll(val[32:], (x + 32 - f + LN) % LN), T)

    def spread(G, x, f):
        return jnp.concatenate([roll(G, (f - x + LN) % LN), roll(G, (f - x - 32 + LN) % LN)], axis=0)

    zero32 = jnp.zeros((32, LN), F32)

    for c in range(2):
        loads[0][c].wait()

        def pack_x(x, T):
            u = packed(st_x, c, x)
            X[pl.ds(pl.multiple_of(c * SYS + x * NR, 8), NR)] = u
            base = pl.multiple_of(c * PSYS + x * PR, 8)
            PB[pl.ds(base, 8)] = jnp.zeros((8, LN), F32)
            PB[pl.ds(base + 72, 8)] = jnp.zeros((8, LN), F32)
            PB[pl.ds(base + 8, NR)] = u
            return pick(T, u, x, zf)
        sxz[c] = lax.fori_loop(0, NP, pack_x, zero32, unroll=4)
        sxy[c] = X[pl.ds(c * SYS + yf, 32, stride=NR)]
    for c in range(2):
        loads[1][c].wait()

        def pack_z(x, T):
            u = packed(st_kz, c, x)
            inner = jnp.where(lanes(NR) % 64 == 63, 0.0, u)
            KZ[pl.ds(pl.multiple_of(c * SYS + x * NR, 8), NR)] = jnp.where(pz == 1, roll(inner, 1), inner)
            return pick(T, u, x, 63)
        skz[c] = lax.fori_loop(0, NP, pack_z, zero32, unroll=4)
    for c in range(2):
        loads[2][c].wait()

        def pack_kx(x, carry):
            u = packed(st_kx, c, x)
            KX[pl.ds(pl.multiple_of(c * SYS + x * NR, 8), NR)] = u
            return carry
        lax.fori_loop(0, NP, pack_kx, 0, unroll=4)
        last = KX[pl.ds(c * SYS + 31 * NR, NR)]
        edge = jnp.logical_and(lanes(NR) >= 64, px == 1)
        KX[pl.ds(c * SYS + 31 * NR, NR)] = jnp.where(edge, 0.0, last)
    for c in range(2):
        loads[3][c].wait()

        def pack_ky(x, carry):
            u = packed(st_ky, c, x)
            rows = lax.broadcasted_iota(jnp.int32, (NR, LN), 0)
            u = jnp.where(jnp.logical_and(rows == NR - 1, py == 1), 0.0, u)
            KY[pl.ds(pl.multiple_of(c * KSYS + x * KR + 8, 8), NR)] = u
            return carry
        lax.fori_loop(0, NP, pack_ky, 0, unroll=4)
        sky[c] = KY[pl.ds(c * KSYS + 71, 32, stride=KR)]

    def remote(src, dst, send_sem, recv_sem, dev):
        return pltpu.make_async_remote_copy(src_ref=src, dst_ref=dst, send_sem=send_sem, recv_sem=recv_sem, device_id=dev, device_id_type=MESH)

    pl.semaphore_wait(barrier, 7)

    def x_plane(ref, c):
        return ref.at[pl.ds(pl.multiple_of(c * SYS + xf * NR, 8), NR)]

    first = []
    for c in range(2):
        first.append([
            remote(sxz.at[c], iz.at[c], isend.at[c, 0], irecv.at[c, 0], nbr['z']),
            remote(sxy.at[c], iy.at[c], isend.at[c, 1], irecv.at[c, 1], nbr['y']),
            remote(x_plane(X, c), ix.at[c], isend.at[c, 2], irecv.at[c, 2], nbr['x']),
            remote(skz.at[c], jz.at[c], isend.at[c, 3], irecv.at[c, 3], nbr['z']),
            remote(sky.at[c], jy.at[c], isend.at[c, 4], irecv.at[c, 4], nbr['y']),
            remote(KX.at[pl.ds(c * SYS + 31 * NR, NR)], jx.at[c], isend.at[c, 5], irecv.at[c, 5], nbr['x'])])
        for cp in first[c]:
            cp.start()

    def reduce_copies(kind, c):
        return [remote(red.at[kind, c, 0], red.at[kind, c, m], dsend.at[kind, c, m], drecv.at[kind, c, m], others[m]) for m in (7, 6, 5, 4, 3, 2, 1)]

    def reduce_start(kind, c, part):
        red[kind, c, 0] = jnp.sum(part, axis=0, keepdims=True)
        for cp in reduce_copies(kind, c):
            cp.start()

    def reduce_end(kind, c):
        for cp in reduce_copies(kind, c):
            cp.wait()
        v = [red[kind, c, m] for m in range(8)]
        total = ((v[0] + v[1]) + (v[2] + v[3])) + ((v[4] + v[5]) + (v[6] + v[7]))
        total = jnp.broadcast_to(total, (8, LN))
        return jnp.broadcast_to(jnp.sum(total, axis=1, keepdims=True), (8, LN))

    def fold(val):
        return jnp.sum(val.reshape(-1, 8, LN), axis=0)

    def wide(vec, n):
        return jnp.broadcast_to(vec[None], (n // 8, 8, LN)).reshape(n, LN)

    def r_copies(c):
        return [
            remote(sz.at[c], rhz.at[c], rsend.at[c, 0], rrecv.at[c, 0], nbr['z']),
            remote(sy.at[c], rhy.at[c], rsend.at[c, 1], rrecv.at[c, 1], nbr['y']),
            remote(x_plane(R, c), rhx.at[c], rsend.at[c, 2], rrecv.at[c, 2], nbr['x'])]

    for c in range(2):
        loads[4][c].wait()
        loads[5][c].wait()
        for cp in first[c]:
            cp.wait()
        lo = splits(NR)
        kx_last = KX[pl.ds(c * SYS + 31 * NR, NR)]
        KXM[c] = roll(jnp.where(lo, kx_last, jnp.where(px == 1, jx[c], 0.0)), 64)
        KY[pl.ds(c * KSYS + 7, 32, stride=KR)] = jnp.where(py == 1, jy[c], 0.0)
        KF[c] = jnp.where(pz == 1, jz[c], skz[c])
        PB[pl.ds(c * PSYS + hrow, 32, stride=PR)] = iy[c]
        u_first = PB[pl.ds(c * PSYS + 8, NR)]
        u_last = PB[pl.ds(c * PSYS + 31 * PR + 8, NR)]
        PB[pl.ds(c * PSYS + 32 * PR + 8, NR)] = roll(jnp.where(lo, ix[c], u_first), 64)
        low = roll(jnp.where(lo, u_last, ix[c]), 64)
        z_flux = KF[c] * (sxz[c] - iz[c])
        kf = KF[c]
        mask = face_mask(NR)

        def start_plane(x, carry):
            T, acc, fx_prev, kx_prev, u = carry
            base = pl.multiple_of(c * PSYS + x * PR, 8)
            at = pl.ds(pl.multiple_of(c * SYS + x * NR, 8), NR)
            kbase = pl.multiple_of(c * KSYS + x * KR, 8)
            nxt = PB[pl.ds(base + PR + 8, NR)]
            yu = PB[pl.ds(base + 9, NR)]
            yl = PB[pl.ds(base + 7, NR)]
            s = packed(st_s, c, x)
            kxv = KX[at]
            kyv = KY[pl.ds(kbase + 8, NR)]
            kyl = KY[pl.ds(kbase + 7, NR)]
            kzv = KZ[at]
            D[at] = s + (kxv + kx_prev) + (kyv + kyl) + (kzv + roll(kzv, fro_z) + jnp.where(mask, spread(kf, x, zf), 0.0))
            fx = kxv * (u - nxt)
            fz = kzv * (u - roll(u, to_z))
            au = s * u + (fx - fx_prev) + (kyv * (u - yu) - kyl * (yl - u)) + (fz - roll(fz, fro_z) + jnp.where(mask, spread(z_flux, x, zf), 0.0))
            r = packed(st_b, c, x) - au
            R[at] = r
            return pick(T, r, x, zf), acc + fold(r * r), fx, kxv, nxt
        T, acc, _, _, _ = lax.fori_loop(0, NP, start_plane, (zero32, jnp.zeros((8, LN), F32), KXM[c] * (low - u_first), KXM[c], u_first), unroll=2)
        reduce_start(0, c, acc)
        sz[c] = T
        sy[c] = R[pl.ds(c * SYS + yf, 32, stride=NR)]
        for cp in r_copies(c):
            cp.start()
        phx[c] = jnp.zeros((NR, LN), F32)
        phy[c] = zero32
        phz[c] = zero32
    hist_s[...] = jnp.zeros((8, LN), F32)
    for c in range(2):
        for cp in r_copies(c):
            cp.wait()

    def q_copies(c, par):
        return [
            remote(sz.at[c], qhz.at[par, c], qsend.at[c, 0], qrecv.at[par, c, 0], nbr['z']),
            remote(sy.at[c], qhy.at[par, c], qsend.at[c, 1], qrecv.at[par, c, 1], nbr['y']),
            remote(x_plane(Q, c), qhx.at[par, c], qsend.at[c, 2], qrecv.at[par, c, 2], nbr['x'])]

    def note(c, k, rho):
        hist_s[...] = jnp.where(jnp.logical_and(lane == k, row8 == c), rho, hist_s[...])

    def product(c, beta):
        b64, b32 = wide(beta, NR), wide(beta, 32)
        hx = rhx[c] + b64 * phx[c]
        hy = rhy[c] + b32 * phy[c]
        hz = rhz[c] + b32 * phz[c]
        phx[c] = hx
        phy[c] = hy
        phz[c] = hz
        PB[pl.ds(c * PSYS + hrow, 32, stride=PR)] = hy
        G = KF[c] * hz
        lo = splits(NR)
        mask = face_mask(NR)

        def direction(x):
            at = pl.ds(c * PSYS + x * PR + 8, NR)
            val = R[pl.ds(c * SYS + x * NR, NR)] + b64 * PB[at]
            PB[at] = val
            return val

        p_first = direction(0)
        p_last = direction(NP - 1)
        above = roll(jnp.where(lo, hx, p_first), 64)
        below = roll(jnp.where(lo, p_last, hx), 64)
        cur, kxp_prev = p_first, KXM[c] * below
        acc, T = jnp.zeros((8, LN), F32), zero32
        for x in range(NP):
            if x + 1 < NP - 1:
                nxt = direction(x + 1)
            elif x + 1 == NP - 1:
                nxt = PB[pl.ds(c * PSYS + (NP - 1) * PR + 8, NR)]
            else:
                nxt = above
            base = c * PSYS + x * PR
            at = pl.ds(c * SYS + x * NR, NR)
            kbase = c * KSYS + x * KR
            kxv, kzv = KX[at], KZ[at]
            kxp = kxv * cur
            zu = jnp.where(mask, spread(G, x, zf), kzv * roll(cur, to_z))
            zl = roll(kzv * cur, fro_z)
            q = D[at] * cur - kxp_prev - kxv * nxt
            q = q - KY[pl.ds(kbase + 8, NR)] * PB[pl.ds(base + 9, NR)]
            q = q - KY[pl.ds(kbase + 7, NR)] * PB[pl.ds(base + 7, NR)]
            q = q - zu - zl
            Q[at] = q
            acc = acc + fold(cur * q)
            T = pick(T, q, x, zf)
            cur, kxp_prev = nxt, kxp
        return acc, T

    CH = 256

    def body(k, carry):
        par = k % 2
        for c in range(2):
            rho = reduce_end(0, c)
            note(c, k, rho)
            beta = jnp.where(k == 0, 0.0, rho / rho_s[c])
            rho_s[c] = rho
            acc, T = product(c, beta)
            reduce_start(1, c, acc)
            sz[c] = T
            sy[c] = Q[pl.ds(c * SYS + yf, 32, stride=NR)]
            for cp in q_copies(c, par):
                cp.start()
        for c in range(2):
            alpha = rho_s[c] / reduce_end(1, c)
            a_ch = wide(alpha, CH)

            def step_r(i, acc):
                at = pl.ds(pl.multiple_of(c * SYS + i * CH, 8), CH)
                r = R[at] - a_ch * Q[at]
                R[at] = r
                return acc + fold(r * r)
            acc = lax.fori_loop(0, SYS // CH, step_r, jnp.zeros((8, LN), F32))
            reduce_start(0, c, acc)

            def step_x(x, carry):
                at = pl.ds(pl.multiple_of(c * SYS + x * NR, 8), NR)
                X[at] = X[at] + wide(alpha, NR) * PB[pl.ds(pl.multiple_of(c * PSYS + x * PR + 8, 8), NR)]
                return carry
            lax.fori_loop(0, NP, step_x, 0, unroll=4)
            for cp in q_copies(c, par):
                cp.wait()
            rhx[c] = rhx[c] - wide(alpha, NR) * qhx[par, c]
            rhy[c] = rhy[c] - wide(alpha, 32) * qhy[par, c]
            rhz[c] = rhz[c] - wide(alpha, 32) * qhz[par, c]
        return carry

    lax.fori_loop(0, ITERS, body, 0)
    for c in range(2):
        note(c, ITERS, reduce_end(0, c))
    hist_out[...] = jnp.sqrt(hist_s[...] * (1.0 / (128 * 128 * 128)))


def run(s, b, x0, kx, ky, kz):
    v = lambda *shape: pltpu.VMEM(shape, F32)
    sem = lambda *shape: pltpu.SemaphoreType.DMA(shape)
    scratch = [v(2, 64, 64, 64)] * 6
    scratch += [v(2 * SYS, LN), v(2 * SYS, LN), v(2 * PSYS, LN), v(2 * SYS, LN), v(2, NR, LN), v(2 * KSYS, LN), v(2 * SYS, LN), v(2 * SYS, LN), v(2, 32, LN)]
    scratch += [v(2, NR, LN), v(2, 32, LN), v(2, 32, LN)] * 2
    scratch += [v(2, 32, LN)] * 6
    scratch += [v(2, NR, LN), v(2, 32, LN), v(2, 32, LN)] * 2
    scratch += [v(2, 2, NR, LN), v(2, 2, 32, LN), v(2, 2, 32, LN)]
    scratch += [v(2, 2, 8, 1, LN), v(2, 8, LN), v(2, 8, LN), v(8, LN)]
    scratch += [sem(6, 2), sem(2, 6), sem(2, 6), sem(2, 3), sem(2, 3), sem(2, 3), sem(2, 2, 3), sem(2, 2, 8), sem(2, 2, 8)]
    xp, hist = pl.pallas_call(
        kernel,
        out_shape=(jax.ShapeDtypeStruct((2 * SYS, LN), F32), jax.ShapeDtypeStruct((8, LN), F32)),
        in_specs=[pl.BlockSpec(memory_space=pl.ANY)] * 6,
        out_specs=(pl.BlockSpec(memory_space=pltpu.VMEM), pl.BlockSpec(memory_space=pltpu.VMEM)),
        scratch_shapes=scratch,
        compiler_params=pltpu.CompilerParams(collective_id=0, has_side_effects=True, vmem_limit_bytes=60 * 1024 * 1024),
        name='cg',
    )(s, b, x0, kx, ky, kz)
    xp = xp.reshape(2, NP, NR, LN)
    x = jnp.concatenate([xp[..., :64], xp[..., 64:]], axis=1)
    return x, hist[:2, :ITERS + 1]


def solution(mesh):
    field = P(None, 'px', 'py', 'pz')
    return jax.shard_map(run, mesh=mesh, in_specs=(field,) * 6, out_specs=(field, P(None, None)), check_vma=False)
```

time: 2720 us -> 227 us (0.08)
  blocking collectives: 991 us -> 0 us
  other arithmetic: 783 us -> 2.57 us
  local copies, waits for them, and re-layouts: 650 us -> 4.22 us
  starting transfers between devices: 280 us -> 0 us
  Pallas kernels: 0 us -> 220 us
    psum x41 -> x0, blocking collectives: 991 us -> none  [global_dot(): return lax.psum(jnp.sum(left_vec * right_vec, axis=(1, 2, 3)), ALL_AXES)]
    reduce_sum x41 -> x0, other arithmetic: 359 us -> none  [global_dot(): return lax.psum(jnp.sum(left_vec * right_vec, axis=(1, 2, 3)), ALL_AXES)]
    slice x106 -> x2, local copies, waits for them, and re-layouts: 362 us -> 4.22 us  [the longest x1 2.97 us: run(): x = jnp.concatenate([xp[..., :64], xp[..., 64:]], axis=1)]
    ppermute x129 -> x0, starting transfers between devices: 280 us -> none  [the longest x63 186 us: neighbour_planes(): from_below = lax.ppermute(last_plane, axis_name, up_pairs(axis_size))]
    mul x61 -> x0, other arithmetic: 224 us -> none  [apply_local(): cond_ext[axis_pos]]
    pallas_call x0 -> x1, Pallas kernels: none -> 220 us  [run(): pl.pallas_call(kernel, out_shape=(jax.ShapeDtypeStruct((2 * SYS, LN), F32...]
    ppermute x43 -> x0, local copies, waits for them, and re-layouts: 194 us -> none  [the longest x21 96.1 us: neighbour_planes(): from_below = lax.ppermute(last_plane, axis_name, up_pairs(axis_size))]
    add x20 -> x0, other arithmetic: 138 us -> none  [cg_step(): direction = res_cur + beta_coef[:, None, None, None] * direction]
  transfers between devices with their start and end apart: 129 -> 0, of which waited for: 0 -> 0; matrix products, arithmetic and copies ran while one was open for 21% -> 0% of each run, Pallas kernels for 0% -> 0%
where the time goes in v1:
time: 227 us
  Pallas kernels  220 us (97%)
  local copies, waits for them, and re-layouts  4.22 us (2%)
  other arithmetic  2.57 us (1%)
    pallas_call x1, Pallas kernels, run(): pl.pallas_call(kernel, out_shape=(jax.ShapeDtypeStruct((2 * SYS, LN), F32...  220 us

profile of v1, /device:TPU:0, one launch (start us, length us, event | category | flops | bytes accessed | tf_op | source)
XLA Modules:
  0.0 227.0 jit_solution(2314665564449262914)
XLA Ops:
  0.6 219.5 %cg.1 = (f32[4096,128]{1,0:T(8,128)}, f32[8,128]{1,0:T(8,128)}) custom-call(f32[2,64,64,64]{3,2,1,0:T(8,128)} %s_hbm.1, f32[2,64,64,64]{3,2,1,0:T(8,128)} %b_hbm.1, f32[2,64,64,64]{3,2,1,0:T(8,128)} %x0_hbm.1, f32[2,64,64,64]{3,2,1,0:T(8,128)} %kx_hbm.1, f32[2,64,64,64]{3,2,1,0:T(8,128)} %ky_hbm.1, f32[2,64,64,64]{3,2,1,0:T(8,128)} %kz_hbm.1), custom_call_target="tpu_custom_call" | custom-call | tf_op jit(solution)/shard_map/cg/pallas_call | solution.py:345
  220.2 1.2 slice.11
  221.4 3.0 %fusion = (f32[2,32,64,64]{3,2,1,0:T(8,128)S(1)}, f32[2,32,64,64]{3,2,1,0:T(8,128)S(1)}) fusion(f32[2,32,64,128]{3,2,1,0:T(8,128)} %bitcast.1), kind=kLoop, calls=%fused_computation.1 | loop fusion | bytes 4194304 | tf_op jit(solution)/shard_map/slice | solution.py:355
  224.4 2.6 %pad_maximum_fusion = f32[2,64,64,64]{3,2,1,0:T(8,128)} fusion(f32[2,32,64,64]{3,2,1,0:T(8,128)S(1)} %get-tuple-element.7, f32[2,32,64,64]{3,2,1,0:T(8,128)S(1)} %get-tuple-element.6), kind=kLoop, calls=%fused_computation | loop fusion | flops 524288 | bytes 4194304 | tf_op jit(solution)/shard_map/concatenate | solution.py:355

commit v2 on v1

--- a/solution.py
+++ b/solution.py
@@ -17,6 +17,7 @@
 SYS = NP * NR
 PSYS = (NP + 1) * PR
 KSYS = NP * KR
+AHEAD = 3
 
 
 def roll(val, shift):
@@ -27,7 +28,7 @@
 
 def kernel(s_hbm, b_hbm, x0_hbm, kx_hbm, ky_hbm, kz_hbm, x_out, hist_out,
            st_s, st_b, st_x, st_kx, st_ky, st_kz,
-           R, Q, PB, KX, KXM, KY, KZ, D, KF,
+           R, Q, PB, KX, KXM, KY, KZ, KZB, D, KF,
            ix, iy, iz, jx, jy, jz, sxy, sxz, sky, skz, sy, sz,
            rhx, rhy, rhz, phx, phy, phz, qhx, qhy, qhz,
            red, rho_s, alpha_s, hist_s,
@@ -101,7 +102,10 @@
         def pack_z(x, T):
             u = packed(st_kz, c, x)
             inner = jnp.where(lanes(NR) % 64 == 63, 0.0, u)
-            KZ[pl.ds(pl.multiple_of(c * SYS + x * NR, 8), NR)] = jnp.where(pz == 1, roll(inner, 1), inner)
+            moved = roll(inner, 1)
+            at = pl.ds(pl.multiple_of(c * SYS + x * NR, 8), NR)
+            KZ[at] = jnp.where(pz == 1, moved, inner)
+            KZB[at] = jnp.where(pz == 1, inner, moved)
             return pick(T, u, x, 63)
         skz[c] = lax.fori_loop(0, NP, pack_z, zero32, unroll=4)
     for c in range(2):
@@ -157,11 +161,15 @@
 
     def reduce_end(kind, c):
         for cp in reduce_copies(kind, c):
-            cp.wait()
+            cp.wait_recv()
         v = [red[kind, c, m] for m in range(8)]
         total = ((v[0] + v[1]) + (v[2] + v[3])) + ((v[4] + v[5]) + (v[6] + v[7]))
         total = jnp.broadcast_to(total, (8, LN))
         return jnp.broadcast_to(jnp.sum(total, axis=1, keepdims=True), (8, LN))
+
+    def reduce_sent(kind, c):
+        for cp in reduce_copies(kind, c):
+            cp.wait_send()
 
     def fold(val):
         return jnp.sum(val.reshape(-1, 8, LN), axis=0)
@@ -207,7 +215,7 @@
             kyv = KY[pl.ds(kbase + 8, NR)]
             kyl = KY[pl.ds(kbase + 7, NR)]
             kzv = KZ[at]
-            D[at] = s + (kxv + kx_prev) + (kyv + kyl) + (kzv + roll(kzv, fro_z) + jnp.where(mask, spread(kf, x, zf), 0.0))
+            D[at] = s + (kxv + kx_prev) + (kyv + kyl) + (kzv + KZB[at] + jnp.where(mask, spread(kf, x, zf), 0.0))
             fx = kxv * (u - nxt)
             fz = kzv * (u - roll(u, to_z))
             au = s * u + (fx - fx_prev) + (kyv * (u - yu) - kyl * (yl - u)) + (fz - roll(fz, fro_z) + jnp.where(mask, spread(z_flux, x, zf), 0.0))
@@ -256,35 +264,41 @@
             PB[at] = val
             return val
 
+        def turn(x, p):
+            at = pl.ds(c * SYS + x * NR, NR)
+            return roll(KZB[at] * p, to_z), roll(KZ[at] * p, fro_z), spread(G, x, zf)
+
+        def load_p(x):
+            return PB[pl.ds(c * PSYS + x * PR + 8, NR)]
+
+        p_last = direction(NP - 1)
         p_first = direction(0)
-        p_last = direction(NP - 1)
         above = roll(jnp.where(lo, hx, p_first), 64)
         below = roll(jnp.where(lo, p_last, hx), 64)
+        turned = {0: turn(0, p_first)}
+        for x in range(1, AHEAD):
+            turned[x] = turn(x, direction(x))
         cur, kxp_prev = p_first, KXM[c] * below
-        acc, T = jnp.zeros((8, LN), F32), zero32
+        acc = jnp.zeros((8, LN), F32)
         for x in range(NP):
-            if x + 1 < NP - 1:
-                nxt = direction(x + 1)
-            elif x + 1 == NP - 1:
-                nxt = PB[pl.ds(c * PSYS + (NP - 1) * PR + 8, NR)]
-            else:
-                nxt = above
+            w = x + AHEAD
+            if w < NP:
+                turned[w] = turn(w, direction(w) if w < NP - 1 else load_p(w))
+            nxt = load_p(x + 1) if x + 1 < NP else above
             base = c * PSYS + x * PR
             at = pl.ds(c * SYS + x * NR, NR)
             kbase = c * KSYS + x * KR
-            kxv, kzv = KX[at], KZ[at]
+            kxv = KX[at]
             kxp = kxv * cur
-            zu = jnp.where(mask, spread(G, x, zf), kzv * roll(cur, to_z))
-            zl = roll(kzv * cur, fro_z)
             q = D[at] * cur - kxp_prev - kxv * nxt
             q = q - KY[pl.ds(kbase + 8, NR)] * PB[pl.ds(base + 9, NR)]
             q = q - KY[pl.ds(kbase + 7, NR)] * PB[pl.ds(base + 7, NR)]
-            q = q - zu - zl
+            zu, zl, e = turned.pop(x)
+            q = q - (jnp.where(mask, e, zu) + zl)
             Q[at] = q
             acc = acc + fold(cur * q)
-            T = pick(T, q, x, zf)
             cur, kxp_prev = nxt, kxp
-        return acc, T
+        return acc
 
     CH = 256
 
@@ -295,14 +309,19 @@
             note(c, k, rho)
             beta = jnp.where(k == 0, 0.0, rho / rho_s[c])
             rho_s[c] = rho
-            acc, T = product(c, beta)
-            reduce_start(1, c, acc)
-            sz[c] = T
+            reduce_start(1, c, product(c, beta))
+        for c in range(2):
+            reduce_sent(0, c)
+
+            def z_face(x, T):
+                return pick(T, Q[pl.ds(pl.multiple_of(c * SYS + x * NR, 8), NR)], x, zf)
+            sz[c] = lax.fori_loop(0, NP, z_face, zero32, unroll=8)
             sy[c] = Q[pl.ds(c * SYS + yf, 32, stride=NR)]
             for cp in q_copies(c, par):
                 cp.start()
         for c in range(2):
             alpha = rho_s[c] / reduce_end(1, c)
+            alpha_s[c] = alpha
             a_ch = wide(alpha, CH)
 
             def step_r(i, acc):
@@ -318,8 +337,11 @@
                 X[at] = X[at] + wide(alpha, NR) * PB[pl.ds(pl.multiple_of(c * PSYS + x * PR + 8, 8), NR)]
                 return carry
             lax.fori_loop(0, NP, step_x, 0, unroll=4)
+        for c in range(2):
+            reduce_sent(1, c)
             for cp in q_copies(c, par):
                 cp.wait()
+            alpha = alpha_s[c]
             rhx[c] = rhx[c] - wide(alpha, NR) * qhx[par, c]
             rhy[c] = rhy[c] - wide(alpha, 32) * qhy[par, c]
             rhz[c] = rhz[c] - wide(alpha, 32) * qhz[par, c]
@@ -328,6 +350,7 @@
     lax.fori_loop(0, ITERS, body, 0)
     for c in range(2):
         note(c, ITERS, reduce_end(0, c))
+        reduce_sent(0, c)
     hist_out[...] = jnp.sqrt(hist_s[...] * (1.0 / (128 * 128 * 128)))
 
 
@@ -335,7 +358,7 @@
     v = lambda *shape: pltpu.VMEM(shape, F32)
     sem = lambda *shape: pltpu.SemaphoreType.DMA(shape)
     scratch = [v(2, 64, 64, 64)] * 6
-    scratch += [v(2 * SYS, LN), v(2 * SYS, LN), v(2 * PSYS, LN), v(2 * SYS, LN), v(2, NR, LN), v(2 * KSYS, LN), v(2 * SYS, LN), v(2 * SYS, LN), v(2, 32, LN)]
+    scratch += [v(2 * SYS, LN), v(2 * SYS, LN), v(2 * PSYS, LN), v(2 * SYS, LN), v(2, NR, LN), v(2 * KSYS, LN), v(2 * SYS, LN), v(2 * SYS, LN), v(2 * SYS, LN), v(2, 32, LN)]
     scratch += [v(2, NR, LN), v(2, 32, LN), v(2, 32, LN)] * 2
     scratch += [v(2, 32, LN)] * 6
     scratch += [v(2, NR, LN), v(2, 32, LN), v(2, 32, LN)] * 2

time: 227 us -> 188 us (0.83)
  Pallas kernels: 220 us -> 180 us
    pallas_call x1, Pallas kernels: 220 us -> 180 us  [run(): pl.pallas_call(kernel, out_shape=(jax.ShapeDtypeStruct((2 * SYS, LN), F32...]
where the time goes in v2:
time: 188 us
  Pallas kernels  180 us (96%)
  local copies, waits for them, and re-layouts  4.22 us (2%)
  other arithmetic  2.57 us (1%)
    pallas_call x1, Pallas kernels, run(): pl.pallas_call(kernel, out_shape=(jax.ShapeDtypeStruct((2 * SYS, LN), F32...  180 us

profile of v2, /device:TPU:0, one launch (start us, length us, event | category | flops | bytes accessed | tf_op | source)
XLA Modules:
  0.0 187.8 jit_solution(13906763534575694409)
XLA Ops:
  0.6 180.3 %cg.1 = (f32[4096,128]{1,0:T(8,128)}, f32[8,128]{1,0:T(8,128)}) custom-call(f32[2,64,64,64]{3,2,1,0:T(8,128)} %s_hbm.1, f32[2,64,64,64]{3,2,1,0:T(8,128)} %b_hbm.1, f32[2,64,64,64]{3,2,1,0:T(8,128)} %x0_hbm.1, f32[2,64,64,64]{3,2,1,0:T(8,128)} %kx_hbm.1, f32[2,64,64,64]{3,2,1,0:T(8,128)} %ky_hbm.1, f32[2,64,64,64]{3,2,1,0:T(8,128)} %kz_hbm.1), custom_call_target="tpu_custom_call" | custom-call | tf_op jit(solution)/shard_map/cg/pallas_call | solution.py:368
  181.0 1.2 slice.11
  182.2 3.0 %fusion = (f32[2,32,64,64]{3,2,1,0:T(8,128)S(1)}, f32[2,32,64,64]{3,2,1,0:T(8,128)S(1)}) fusion(f32[2,32,64,128]{3,2,1,0:T(8,128)} %bitcast.1), kind=kLoop, calls=%fused_computation.1 | loop fusion | bytes 4194304 | tf_op jit(solution)/shard_map/slice | solution.py:378
  185.2 2.6 %pad_maximum_fusion = f32[2,64,64,64]{3,2,1,0:T(8,128)} fusion(f32[2,32,64,64]{3,2,1,0:T(8,128)S(1)} %get-tuple-element.7, f32[2,32,64,64]{3,2,1,0:T(8,128)S(1)} %get-tuple-element.6), kind=kLoop, calls=%fused_computation | loop fusion | flops 524288 | bytes 4194304 | tf_op jit(solution)/shard_map/concatenate | solution.py:378

commit v3 on v2

--- a/solution.py
+++ b/solution.py
@@ -52,6 +52,7 @@
     hrow = 72 - 65 * py
     to_z = 127 - 126 * pz
     fro_z = 1 + 126 * pz
+    zturn = 63 + 65 * pz
 
     def face_mask(n):
         return (lanes(n) % 64) == zf
@@ -62,9 +63,10 @@
     loads = []
     for num, (src, dst) in enumerate(((x0_hbm, st_x), (kz_hbm, st_kz), (kx_hbm, st_kx), (ky_hbm, st_ky), (s_hbm, st_s), (b_hbm, st_b))):
         pair = [pltpu.make_async_copy(src.at[c], dst.at[c], ld_sem.at[num, c]) for c in range(2)]
-        for cp in pair:
+        loads.append(pair)
+    for num in range(2):
+        for cp in loads[num]:
             cp.start()
-        loads.append(pair)
 
     barrier = pltpu.get_barrier_semaphore()
     for m in range(1, 8):
@@ -75,16 +77,19 @@
 
     def pick(T, val, x, f):
         l64 = lanes(32) % 64
-        T = jnp.where(l64 == x, roll(val[:32], (x - f + LN) % LN), T)
-        return jnp.where(l64 == x + 32, roll(val[32:], (x + 32 - f + LN) % LN), T)
+        T = jnp.where(l64 == x, roll(val[:32], lax.rem(x - f + LN, LN)), T)
+        return jnp.where(l64 == x + 32, roll(val[32:], lax.rem(x + 32 - f + LN, LN)), T)
 
     def spread(G, x, f):
-        return jnp.concatenate([roll(G, (f - x + LN) % LN), roll(G, (f - x - 32 + LN) % LN)], axis=0)
+        return jnp.concatenate([roll(G, lax.rem(f - x + LN, LN)), roll(G, lax.rem(f - x - 32 + LN, LN))], axis=0)
 
     zero32 = jnp.zeros((32, LN), F32)
 
     for c in range(2):
         loads[0][c].wait()
+        for num in ((2,), (3, 4, 5))[c]:
+            for cp in loads[num]:
+                cp.start()
 
         def pack_x(x, T):
             u = packed(st_x, c, x)
@@ -94,7 +99,7 @@
             PB[pl.ds(base + 72, 8)] = jnp.zeros((8, LN), F32)
             PB[pl.ds(base + 8, NR)] = u
             return pick(T, u, x, zf)
-        sxz[c] = lax.fori_loop(0, NP, pack_x, zero32, unroll=4)
+        sxz[c] = lax.fori_loop(0, NP, pack_x, zero32, unroll=8)
         sxy[c] = X[pl.ds(c * SYS + yf, 32, stride=NR)]
     for c in range(2):
         loads[1][c].wait()
@@ -107,7 +112,7 @@
             KZ[at] = jnp.where(pz == 1, moved, inner)
             KZB[at] = jnp.where(pz == 1, inner, moved)
             return pick(T, u, x, 63)
-        skz[c] = lax.fori_loop(0, NP, pack_z, zero32, unroll=4)
+        skz[c] = lax.fori_loop(0, NP, pack_z, zero32, unroll=8)
     for c in range(2):
         loads[2][c].wait()
 
@@ -115,7 +120,7 @@
             u = packed(st_kx, c, x)
             KX[pl.ds(pl.multiple_of(c * SYS + x * NR, 8), NR)] = u
             return carry
-        lax.fori_loop(0, NP, pack_kx, 0, unroll=4)
+        lax.fori_loop(0, NP, pack_kx, 0, unroll=8)
         last = KX[pl.ds(c * SYS + 31 * NR, NR)]
         edge = jnp.logical_and(lanes(NR) >= 64, px == 1)
         KX[pl.ds(c * SYS + 31 * NR, NR)] = jnp.where(edge, 0.0, last)
@@ -128,7 +133,7 @@
             u = jnp.where(jnp.logical_and(rows == NR - 1, py == 1), 0.0, u)
             KY[pl.ds(pl.multiple_of(c * KSYS + x * KR + 8, 8), NR)] = u
             return carry
-        lax.fori_loop(0, NP, pack_ky, 0, unroll=4)
+        lax.fori_loop(0, NP, pack_ky, 0, unroll=8)
         sky[c] = KY[pl.ds(c * KSYS + 71, 32, stride=KR)]
 
     def remote(src, dst, send_sem, recv_sem, dev):
@@ -222,7 +227,7 @@
             r = packed(st_b, c, x) - au
             R[at] = r
             return pick(T, r, x, zf), acc + fold(r * r), fx, kxv, nxt
-        T, acc, _, _, _ = lax.fori_loop(0, NP, start_plane, (zero32, jnp.zeros((8, LN), F32), KXM[c] * (low - u_first), KXM[c], u_first), unroll=2)
+        T, acc, _, _, _ = lax.fori_loop(0, NP, start_plane, (zero32, jnp.zeros((8, LN), F32), KXM[c] * (low - u_first), KXM[c], u_first), unroll=4)
         reduce_start(0, c, acc)
         sz[c] = T
         sy[c] = R[pl.ds(c * SYS + yf, 32, stride=NR)]
@@ -266,7 +271,8 @@
 
         def turn(x, p):
             at = pl.ds(c * SYS + x * NR, NR)
-            return roll(KZB[at] * p, to_z), roll(KZ[at] * p, fro_z), spread(G, x, zf)
+            e = jnp.concatenate([roll(G, zf if x == 0 else zturn - x), roll(G, zturn - x - 32)], axis=0)
+            return roll(KZB[at] * p, to_z), roll(KZ[at] * p, fro_z), e
 
         def load_p(x):
             return PB[pl.ds(c * PSYS + x * PR + 8, NR)]
@@ -354,6 +360,37 @@
     hist_out[...] = jnp.sqrt(hist_s[...] * (1.0 / (128 * 128 * 128)))
 
 
+CHUNKS = 2
+VMEM_MAIN = 60 * 1024 * 1024
+
+
+def unpack(xp, hist, x_out, hist_out, buf, st, in_sem, out_sem):
+    planes = NP // CHUNKS
+    loads = []
+    for n in range(2 * CHUNKS):
+        at = pl.ds(n * planes * NR, planes * NR)
+        loads.append(pltpu.make_async_copy(xp.at[at], buf.at[at], in_sem.at[n]))
+        loads[n].start()
+    hist_out[...] = hist[:2, :ITERS + 1]
+    stores = []
+    for n in range(2 * CHUNKS):
+        c, x0 = n // CHUNKS, n % CHUNKS * planes
+        loads[n].wait()
+
+        def plane(x, carry):
+            val = buf[pl.ds(pl.multiple_of(n * planes * NR + x * NR, 8), NR)]
+            st[c, x0 + x] = val[:, :64]
+            st[c, x0 + x + NP] = roll(val, 64)[:, :64]
+            return carry
+        lax.fori_loop(0, planes, plane, 0, unroll=8)
+        for h in range(2):
+            at = pl.ds(x0 + NP * h, planes)
+            stores.append(pltpu.make_async_copy(st.at[c, at], x_out.at[c, at], out_sem.at[n, h]))
+            stores[-1].start()
+    for cp in stores:
+        cp.wait()
+
+
 def run(s, b, x0, kx, ky, kz):
     v = lambda *shape: pltpu.VMEM(shape, F32)
     sem = lambda *shape: pltpu.SemaphoreType.DMA(shape)
@@ -371,12 +408,18 @@
         in_specs=[pl.BlockSpec(memory_space=pl.ANY)] * 6,
         out_specs=(pl.BlockSpec(memory_space=pltpu.VMEM), pl.BlockSpec(memory_space=pltpu.VMEM)),
         scratch_shapes=scratch,
-        compiler_params=pltpu.CompilerParams(collective_id=0, has_side_effects=True, vmem_limit_bytes=60 * 1024 * 1024),
+        compiler_params=pltpu.CompilerParams(collective_id=0, has_side_effects=True, vmem_limit_bytes=VMEM_MAIN),
         name='cg',
     )(s, b, x0, kx, ky, kz)
-    xp = xp.reshape(2, NP, NR, LN)
-    x = jnp.concatenate([xp[..., :64], xp[..., 64:]], axis=1)
-    return x, hist[:2, :ITERS + 1]
+    return pl.pallas_call(
+        unpack,
+        out_shape=(jax.ShapeDtypeStruct((2, 64, 64, 64), F32), jax.ShapeDtypeStruct((2, ITERS + 1), F32)),
+        in_specs=[pl.BlockSpec(memory_space=pl.ANY), pl.BlockSpec(memory_space=pltpu.VMEM)],
+        out_specs=(pl.BlockSpec(memory_space=pl.ANY), pl.BlockSpec(memory_space=pltpu.VMEM)),
+        scratch_shapes=[v(2 * SYS, LN), v(2, 64, 64, 64), sem(2 * CHUNKS), sem(2 * CHUNKS, 2)],
+        compiler_params=pltpu.CompilerParams(vmem_limit_bytes=60 * 1024 * 1024),
+        name='unpack',
+    )(xp, hist)
 
 
 def solution(mesh):

time: 188 us -> 184 us (0.979)
  local copies, waits for them, and re-layouts: 4.22 us -> 0 us
  Pallas kernels: 180 us -> 183 us
  other arithmetic: 2.57 us -> 0 us
    pallas_call x0 -> x1, Pallas kernels: none -> 4.66 us  [run(): pl.pallas_call(unpack, out_shape=(jax.ShapeDtypeStruct((2, 64, 64, 64), F...]
    slice x2 -> x0, local copies, waits for them, and re-layouts: 4.22 us -> none  [the longest x1 2.97 us: run(): x = jnp.concatenate([xp[..., :64], xp[..., 64:]], axis=1)]
    concatenate x1 -> x0, other arithmetic: 2.57 us -> none  [run(): x = jnp.concatenate([xp[..., :64], xp[..., 64:]], axis=1)]
    pallas_call x1, Pallas kernels: 180 us -> 178 us  [run(): pl.pallas_call(kernel, out_shape=(jax.ShapeDtypeStruct((2 * SYS, LN), F32...]
where the time goes in v3:
time: 184 us; the launch traced here: 183 us
  Pallas kernels  183 us (99%)
    pallas_call x1, Pallas kernels, run(): pl.pallas_call(kernel, out_shape=(jax.ShapeDtypeStruct((2 * SYS, LN), F32...  178 us
    pallas_call x1, Pallas kernels, run(): pl.pallas_call(unpack, out_shape=(jax.ShapeDtypeStruct((2, 64, 64, 64), F...  4.66 us

profile of v3, /device:TPU:0, one launch (start us, length us, event | category | flops | bytes accessed | tf_op | source)
XLA Modules:
  0.0 183.5 jit_solution(12602768740303198154)
XLA Ops:
  0.6 178.2 %cg.1 = (f32[4096,128]{1,0:T(8,128)}, f32[8,128]{1,0:T(8,128)}) custom-call(f32[2,64,64,64]{3,2,1,0:T(8,128)} %s_hbm.1, f32[2,64,64,64]{3,2,1,0:T(8,128)} %b_hbm.1, f32[2,64,64,64]{3,2,1,0:T(8,128)} %x0_hbm.1, f32[2,64,64,64]{3,2,1,0:T(8,128)} %kx_hbm.1, f32[2,64,64,64]{3,2,1,0:T(8,128)} %ky_hbm.1, f32[2,64,64,64]{3,2,1,0:T(8,128)} %kz_hbm.1), custom_call_target="tpu_custom_call" | custom-call | tf_op jit(solution)/shard_map/cg/pallas_call | solution.py:405
  178.8 4.7 %unpack.1 = (f32[2,64,64,64]{3,2,1,0:T(8,128)}, f32[2,21]{1,0:T(2,128)}) custom-call(f32[4096,128]{1,0:T(8,128)} %get-tuple-element.4.xp, f32[8,128]{1,0:T(8,128)} %get-tuple-element.5.hist), custom_call_target="tpu_custom_call" | custom-call | tf_op jit(solution)/shard_map/unpack/pallas_call | solution.py:414

commit v4 on v3

--- a/solution.py
+++ b/solution.py
@@ -28,12 +28,11 @@
 
 def kernel(s_hbm, b_hbm, x0_hbm, kx_hbm, ky_hbm, kz_hbm, x_out, hist_out,
            st_s, st_b, st_x, st_kx, st_ky, st_kz,
-           R, Q, PB, KX, KXM, KY, KZ, KZB, D, KF,
+           X, R, Q, PB, PZ, RZ, KX, KXM, KY, KZ, KZF, D, KF,
            ix, iy, iz, jx, jy, jz, sxy, sxz, sky, skz, sy, sz,
-           rhx, rhy, rhz, phx, phy, phz, qhx, qhy, qhz,
+           rhx, rhy, rhz, phx, phy, qhx, qhy, qhz,
            red, rho_s, alpha_s, hist_s,
-           ld_sem, isend, irecv, rsend, rrecv, qsend, qrecv, dsend, drecv):
-    X = x_out
+           ld_sem, isend, irecv, rsend, rrecv, qsend, qrecv, dsend, drecv, out_sem):
     pz, py, px = lax.axis_index('pz'), lax.axis_index('py'), lax.axis_index('px')
     nbr = {'x': (pz, py, 1 - px), 'y': (pz, 1 - py, px), 'z': (1 - pz, py, px)}
     others = {}
@@ -52,7 +51,6 @@
     hrow = 72 - 65 * py
     to_z = 127 - 126 * pz
     fro_z = 1 + 126 * pz
-    zturn = 63 + 65 * pz
 
     def face_mask(n):
         return (lanes(n) % 64) == zf
@@ -64,7 +62,7 @@
     for num, (src, dst) in enumerate(((x0_hbm, st_x), (kz_hbm, st_kz), (kx_hbm, st_kx), (ky_hbm, st_ky), (s_hbm, st_s), (b_hbm, st_b))):
         pair = [pltpu.make_async_copy(src.at[c], dst.at[c], ld_sem.at[num, c]) for c in range(2)]
         loads.append(pair)
-    for num in range(2):
+    for num in range(1):
         for cp in loads[num]:
             cp.start()
 
@@ -85,15 +83,34 @@
 
     zero32 = jnp.zeros((32, LN), F32)
 
+    def remote(src, dst, send_sem, recv_sem, dev):
+        return pltpu.make_async_remote_copy(src_ref=src, dst_ref=dst, send_sem=send_sem, recv_sem=recv_sem, device_id=dev, device_id_type=MESH)
+
+    def x_plane(ref, c):
+        return ref.at[pl.ds(pl.multiple_of(c * SYS + xf * NR, 8), NR)]
+
+    def rows(x, c):
+        return pl.ds(pl.multiple_of(c * SYS + x * NR, 8), NR)
+
+    first = []
+    for c in range(2):
+        first.append([
+            remote(sxz.at[c], iz.at[c], isend.at[c, 0], irecv.at[c, 0], nbr['z']),
+            remote(sxy.at[c], iy.at[c], isend.at[c, 1], irecv.at[c, 1], nbr['y']),
+            remote(x_plane(X, c), ix.at[c], isend.at[c, 2], irecv.at[c, 2], nbr['x']),
+            remote(skz.at[c], jz.at[c], isend.at[c, 3], irecv.at[c, 3], nbr['z']),
+            remote(sky.at[c], jy.at[c], isend.at[c, 4], irecv.at[c, 4], nbr['y']),
+            remote(KX.at[pl.ds(c * SYS + 31 * NR, NR)], jx.at[c], isend.at[c, 5], irecv.at[c, 5], nbr['x'])])
+
     for c in range(2):
         loads[0][c].wait()
-        for num in ((2,), (3, 4, 5))[c]:
+        for num in ((1, 2), (3, 4, 5))[c]:
             for cp in loads[num]:
                 cp.start()
 
         def pack_x(x, T):
             u = packed(st_x, c, x)
-            X[pl.ds(pl.multiple_of(c * SYS + x * NR, 8), NR)] = u
+            X[rows(x, c)] = u
             base = pl.multiple_of(c * PSYS + x * PR, 8)
             PB[pl.ds(base, 8)] = jnp.zeros((8, LN), F32)
             PB[pl.ds(base + 72, 8)] = jnp.zeros((8, LN), F32)
@@ -101,6 +118,10 @@
             return pick(T, u, x, zf)
         sxz[c] = lax.fori_loop(0, NP, pack_x, zero32, unroll=8)
         sxy[c] = X[pl.ds(c * SYS + yf, 32, stride=NR)]
+    pl.semaphore_wait(barrier, 7)
+    for c in range(2):
+        for cp in first[c][:3]:
+            cp.start()
     for c in range(2):
         loads[1][c].wait()
 
@@ -108,53 +129,45 @@
             u = packed(st_kz, c, x)
             inner = jnp.where(lanes(NR) % 64 == 63, 0.0, u)
             moved = roll(inner, 1)
-            at = pl.ds(pl.multiple_of(c * SYS + x * NR, 8), NR)
-            KZ[at] = jnp.where(pz == 1, moved, inner)
-            KZB[at] = jnp.where(pz == 1, inner, moved)
+            KZ[rows(x, c)] = jnp.where(pz == 1, moved, inner)
+            KZF[rows(x, c)] = jnp.where(pz == 1, inner, moved)
             return pick(T, u, x, 63)
         skz[c] = lax.fori_loop(0, NP, pack_z, zero32, unroll=8)
     for c in range(2):
         loads[2][c].wait()
 
         def pack_kx(x, carry):
-            u = packed(st_kx, c, x)
-            KX[pl.ds(pl.multiple_of(c * SYS + x * NR, 8), NR)] = u
+            KX[rows(x, c)] = packed(st_kx, c, x)
             return carry
         lax.fori_loop(0, NP, pack_kx, 0, unroll=8)
         last = KX[pl.ds(c * SYS + 31 * NR, NR)]
         edge = jnp.logical_and(lanes(NR) >= 64, px == 1)
         KX[pl.ds(c * SYS + 31 * NR, NR)] = jnp.where(edge, 0.0, last)
+        first[c][3].start()
     for c in range(2):
         loads[3][c].wait()
 
         def pack_ky(x, carry):
             u = packed(st_ky, c, x)
-            rows = lax.broadcasted_iota(jnp.int32, (NR, LN), 0)
-            u = jnp.where(jnp.logical_and(rows == NR - 1, py == 1), 0.0, u)
+            row = lax.broadcasted_iota(jnp.int32, (NR, LN), 0)
+            u = jnp.where(jnp.logical_and(row == NR - 1, py == 1), 0.0, u)
             KY[pl.ds(pl.multiple_of(c * KSYS + x * KR + 8, 8), NR)] = u
             return carry
         lax.fori_loop(0, NP, pack_ky, 0, unroll=8)
         sky[c] = KY[pl.ds(c * KSYS + 71, 32, stride=KR)]
-
-    def remote(src, dst, send_sem, recv_sem, dev):
-        return pltpu.make_async_remote_copy(src_ref=src, dst_ref=dst, send_sem=send_sem, recv_sem=recv_sem, device_id=dev, device_id_type=MESH)
-
-    pl.semaphore_wait(barrier, 7)
-
-    def x_plane(ref, c):
-        return ref.at[pl.ds(pl.multiple_of(c * SYS + xf * NR, 8), NR)]
-
-    first = []
-    for c in range(2):
-        first.append([
-            remote(sxz.at[c], iz.at[c], isend.at[c, 0], irecv.at[c, 0], nbr['z']),
-            remote(sxy.at[c], iy.at[c], isend.at[c, 1], irecv.at[c, 1], nbr['y']),
-            remote(x_plane(X, c), ix.at[c], isend.at[c, 2], irecv.at[c, 2], nbr['x']),
-            remote(skz.at[c], jz.at[c], isend.at[c, 3], irecv.at[c, 3], nbr['z']),
-            remote(sky.at[c], jy.at[c], isend.at[c, 4], irecv.at[c, 4], nbr['y']),
-            remote(KX.at[pl.ds(c * SYS + 31 * NR, NR)], jx.at[c], isend.at[c, 5], irecv.at[c, 5], nbr['x'])])
-        for cp in first[c]:
-            cp.start()
+        first[c][5].start()
+    for c in range(2):
+        loads[4][c].wait()
+        loads[5][c].wait()
+        if c == 0:
+            for cp in (first[0][4], first[1][4]):
+                cp.start()
+
+        def pack_sb(x, carry):
+            D[rows(x, c)] = packed(st_s, c, x)
+            R[rows(x, c)] = packed(st_b, c, x)
+            return carry
+        lax.fori_loop(0, NP, pack_sb, 0, unroll=8)
 
     def reduce_copies(kind, c):
         return [remote(red.at[kind, c, 0], red.at[kind, c, m], dsend.at[kind, c, m], drecv.at[kind, c, m], others[m]) for m in (7, 6, 5, 4, 3, 2, 1)]
@@ -189,8 +202,6 @@
             remote(x_plane(R, c), rhx.at[c], rsend.at[c, 2], rrecv.at[c, 2], nbr['x'])]
 
     for c in range(2):
-        loads[4][c].wait()
-        loads[5][c].wait()
         for cp in first[c]:
             cp.wait()
         lo = splits(NR)
@@ -203,43 +214,61 @@
         u_last = PB[pl.ds(c * PSYS + 31 * PR + 8, NR)]
         PB[pl.ds(c * PSYS + 32 * PR + 8, NR)] = roll(jnp.where(lo, ix[c], u_first), 64)
         low = roll(jnp.where(lo, u_last, ix[c]), 64)
-        z_flux = KF[c] * (sxz[c] - iz[c])
-        kf = KF[c]
+        kf, uf = KF[c], iz[c]
         mask = face_mask(NR)
 
         def start_plane(x, carry):
-            T, acc, fx_prev, kx_prev, u = carry
+            acc, fx_prev, kx_prev, u = carry
             base = pl.multiple_of(c * PSYS + x * PR, 8)
-            at = pl.ds(pl.multiple_of(c * SYS + x * NR, 8), NR)
+            at = rows(x, c)
             kbase = pl.multiple_of(c * KSYS + x * KR, 8)
             nxt = PB[pl.ds(base + PR + 8, NR)]
             yu = PB[pl.ds(base + 9, NR)]
             yl = PB[pl.ds(base + 7, NR)]
-            s = packed(st_s, c, x)
+            s = D[at]
             kxv = KX[at]
             kyv = KY[pl.ds(kbase + 8, NR)]
             kyl = KY[pl.ds(kbase + 7, NR)]
-            kzv = KZ[at]
-            D[at] = s + (kxv + kx_prev) + (kyv + kyl) + (kzv + KZB[at] + jnp.where(mask, spread(kf, x, zf), 0.0))
+            kzf = jnp.where(mask, spread(kf, x, zf), KZ[at])
+            uz = jnp.where(mask, spread(uf, x, zf), roll(u, to_z))
             fx = kxv * (u - nxt)
-            fz = kzv * (u - roll(u, to_z))
-            au = s * u + (fx - fx_prev) + (kyv * (u - yu) - kyl * (yl - u)) + (fz - roll(fz, fro_z) + jnp.where(mask, spread(z_flux, x, zf), 0.0))
-            r = packed(st_b, c, x) - au
+            fz = kzf * (u - uz)
+            fz_away = roll(jnp.where(mask, 0.0, fz), fro_z)
+            D[at] = s + (kxv + kx_prev) + (kyv + kyl) + (kzf + KZF[at])
+            KZF[at] = kzf
+            PZ[at] = uz
+            r = R[at] - (s * u + (fx - fx_prev) + (kyv * (u - yu) - kyl * (yl - u)) + (fz - fz_away))
             R[at] = r
-            return pick(T, r, x, zf), acc + fold(r * r), fx, kxv, nxt
-        T, acc, _, _, _ = lax.fori_loop(0, NP, start_plane, (zero32, jnp.zeros((8, LN), F32), KXM[c] * (low - u_first), KXM[c], u_first), unroll=4)
+            return acc + fold(r * r), fx, kxv, nxt
+        acc, _, _, _ = lax.fori_loop(0, NP, start_plane, (jnp.zeros((8, LN), F32), KXM[c] * (low - u_first), KXM[c], u_first), unroll=4)
         reduce_start(0, c, acc)
-        sz[c] = T
-        sy[c] = R[pl.ds(c * SYS + yf, 32, stride=NR)]
+
+    def z_face(ref, c):
+        def plane(x, T):
+            return pick(T, ref[rows(x, c)], x, zf)
+        sz[c] = lax.fori_loop(0, NP, plane, zero32, unroll=8)
+        sy[c] = ref[pl.ds(c * SYS + yf, 32, stride=NR)]
+
+    def turn_r(c):
+        G = rhz[c]
+        mask = face_mask(NR)
+
+        def plane(x, carry):
+            RZ[rows(x, c)] = jnp.where(mask, spread(G, x, zf), roll(R[rows(x, c)], to_z))
+            return carry
+        lax.fori_loop(0, NP, plane, 0, unroll=8)
+
+    for c in range(2):
+        z_face(R, c)
         for cp in r_copies(c):
             cp.start()
         phx[c] = jnp.zeros((NR, LN), F32)
         phy[c] = zero32
-        phz[c] = zero32
     hist_s[...] = jnp.zeros((8, LN), F32)
     for c in range(2):
         for cp in r_copies(c):
             cp.wait()
+        turn_r(c)
 
     def q_copies(c, par):
         return [
@@ -251,17 +280,13 @@
         hist_s[...] = jnp.where(jnp.logical_and(lane == k, row8 == c), rho, hist_s[...])
 
     def product(c, beta):
-        b64, b32 = wide(beta, NR), wide(beta, 32)
+        b64 = wide(beta, NR)
         hx = rhx[c] + b64 * phx[c]
-        hy = rhy[c] + b32 * phy[c]
-        hz = rhz[c] + b32 * phz[c]
+        hy = rhy[c] + wide(beta, 32) * phy[c]
         phx[c] = hx
         phy[c] = hy
-        phz[c] = hz
         PB[pl.ds(c * PSYS + hrow, 32, stride=PR)] = hy
-        G = KF[c] * hz
         lo = splits(NR)
-        mask = face_mask(NR)
 
         def direction(x):
             at = pl.ds(c * PSYS + x * PR + 8, NR)
@@ -270,9 +295,7 @@
             return val
 
         def turn(x, p):
-            at = pl.ds(c * SYS + x * NR, NR)
-            e = jnp.concatenate([roll(G, zf if x == 0 else zturn - x), roll(G, zturn - x - 32)], axis=0)
-            return roll(KZB[at] * p, to_z), roll(KZ[at] * p, fro_z), e
+            return roll(KZ[pl.ds(c * SYS + x * NR, NR)] * p, fro_z)
 
         def load_p(x):
             return PB[pl.ds(c * PSYS + x * PR + 8, NR)]
@@ -299,14 +322,15 @@
             q = D[at] * cur - kxp_prev - kxv * nxt
             q = q - KY[pl.ds(kbase + 8, NR)] * PB[pl.ds(base + 9, NR)]
             q = q - KY[pl.ds(kbase + 7, NR)] * PB[pl.ds(base + 7, NR)]
-            zu, zl, e = turned.pop(x)
-            q = q - (jnp.where(mask, e, zu) + zl)
+            pz_new = RZ[at] + b64 * PZ[at]
+            PZ[at] = pz_new
+            q = q - KZF[at] * pz_new - turned.pop(x)
             Q[at] = q
             acc = acc + fold(cur * q)
             cur, kxp_prev = nxt, kxp
         return acc
 
-    CH = 256
+    CH = 512
 
     def body(k, carry):
         par = k % 2
@@ -319,10 +343,7 @@
         for c in range(2):
             reduce_sent(0, c)
 
-            def z_face(x, T):
-                return pick(T, Q[pl.ds(pl.multiple_of(c * SYS + x * NR, 8), NR)], x, zf)
-            sz[c] = lax.fori_loop(0, NP, z_face, zero32, unroll=8)
-            sy[c] = Q[pl.ds(c * SYS + yf, 32, stride=NR)]
+            z_face(Q, c)
             for cp in q_copies(c, par):
                 cp.start()
         for c in range(2):
@@ -351,27 +372,34 @@
             rhx[c] = rhx[c] - wide(alpha, NR) * qhx[par, c]
             rhy[c] = rhy[c] - wide(alpha, 32) * qhy[par, c]
             rhz[c] = rhz[c] - wide(alpha, 32) * qhz[par, c]
+            turn_r(c)
         return carry
 
     lax.fori_loop(0, ITERS, body, 0)
+    outs = [pltpu.make_async_copy(X.at[pl.ds(c * SYS, SYS)], x_out.at[pl.ds(c * SYS, SYS)], out_sem.at[c]) for c in range(2)]
+    for cp in outs:
+        cp.start()
     for c in range(2):
         note(c, ITERS, reduce_end(0, c))
         reduce_sent(0, c)
     hist_out[...] = jnp.sqrt(hist_s[...] * (1.0 / (128 * 128 * 128)))
+    for cp in outs:
+        cp.wait()
 
 
 CHUNKS = 2
 VMEM_MAIN = 60 * 1024 * 1024
 
 
-def unpack(xp, hist, x_out, hist_out, buf, st, in_sem, out_sem):
+def unpack(xp, hist, x_out, hist_out, buf, st, hs, ho, in_sem, out_sem, h_sem):
     planes = NP // CHUNKS
+    hist_in = pltpu.make_async_copy(hist, hs, h_sem.at[0])
+    hist_in.start()
     loads = []
     for n in range(2 * CHUNKS):
         at = pl.ds(n * planes * NR, planes * NR)
         loads.append(pltpu.make_async_copy(xp.at[at], buf.at[at], in_sem.at[n]))
         loads[n].start()
-    hist_out[...] = hist[:2, :ITERS + 1]
     stores = []
     for n in range(2 * CHUNKS):
         c, x0 = n // CHUNKS, n % CHUNKS * planes
@@ -382,11 +410,15 @@
             st[c, x0 + x] = val[:, :64]
             st[c, x0 + x + NP] = roll(val, 64)[:, :64]
             return carry
-        lax.fori_loop(0, planes, plane, 0, unroll=8)
+        lax.fori_loop(0, planes, plane, 0, unroll=16)
         for h in range(2):
             at = pl.ds(x0 + NP * h, planes)
             stores.append(pltpu.make_async_copy(st.at[c, at], x_out.at[c, at], out_sem.at[n, h]))
             stores[-1].start()
+    hist_in.wait()
+    ho[...] = hs[:2, :ITERS + 1]
+    stores.append(pltpu.make_async_copy(ho, hist_out, h_sem.at[1]))
+    stores[-1].start()
     for cp in stores:
         cp.wait()
 
@@ -395,18 +427,19 @@
     v = lambda *shape: pltpu.VMEM(shape, F32)
     sem = lambda *shape: pltpu.SemaphoreType.DMA(shape)
     scratch = [v(2, 64, 64, 64)] * 6
-    scratch += [v(2 * SYS, LN), v(2 * SYS, LN), v(2 * PSYS, LN), v(2 * SYS, LN), v(2, NR, LN), v(2 * KSYS, LN), v(2 * SYS, LN), v(2 * SYS, LN), v(2 * SYS, LN), v(2, 32, LN)]
+    full = v(2 * SYS, LN)
+    scratch += [full, full, full, v(2 * PSYS, LN), full, full, full, v(2, NR, LN), v(2 * KSYS, LN), full, full, full, v(2, 32, LN)]
     scratch += [v(2, NR, LN), v(2, 32, LN), v(2, 32, LN)] * 2
     scratch += [v(2, 32, LN)] * 6
-    scratch += [v(2, NR, LN), v(2, 32, LN), v(2, 32, LN)] * 2
+    scratch += [v(2, NR, LN), v(2, 32, LN), v(2, 32, LN), v(2, NR, LN), v(2, 32, LN)]
     scratch += [v(2, 2, NR, LN), v(2, 2, 32, LN), v(2, 2, 32, LN)]
     scratch += [v(2, 2, 8, 1, LN), v(2, 8, LN), v(2, 8, LN), v(8, LN)]
-    scratch += [sem(6, 2), sem(2, 6), sem(2, 6), sem(2, 3), sem(2, 3), sem(2, 3), sem(2, 2, 3), sem(2, 2, 8), sem(2, 2, 8)]
+    scratch += [sem(6, 2), sem(2, 6), sem(2, 6), sem(2, 3), sem(2, 3), sem(2, 3), sem(2, 2, 3), sem(2, 2, 8), sem(2, 2, 8), sem(2)]
     xp, hist = pl.pallas_call(
         kernel,
         out_shape=(jax.ShapeDtypeStruct((2 * SYS, LN), F32), jax.ShapeDtypeStruct((8, LN), F32)),
         in_specs=[pl.BlockSpec(memory_space=pl.ANY)] * 6,
-        out_specs=(pl.BlockSpec(memory_space=pltpu.VMEM), pl.BlockSpec(memory_space=pltpu.VMEM)),
+        out_specs=(pl.BlockSpec(memory_space=pl.ANY), pl.BlockSpec(memory_space=pltpu.VMEM)),
         scratch_shapes=scratch,
         compiler_params=pltpu.CompilerParams(collective_id=0, has_side_effects=True, vmem_limit_bytes=VMEM_MAIN),
         name='cg',
@@ -414,9 +447,9 @@
     return pl.pallas_call(
         unpack,
         out_shape=(jax.ShapeDtypeStruct((2, 64, 64, 64), F32), jax.ShapeDtypeStruct((2, ITERS + 1), F32)),
-        in_specs=[pl.BlockSpec(memory_space=pl.ANY), pl.BlockSpec(memory_space=pltpu.VMEM)],
-        out_specs=(pl.BlockSpec(memory_space=pl.ANY), pl.BlockSpec(memory_space=pltpu.VMEM)),
-        scratch_shapes=[v(2 * SYS, LN), v(2, 64, 64, 64), sem(2 * CHUNKS), sem(2 * CHUNKS, 2)],
+        in_specs=[pl.BlockSpec(memory_space=pl.ANY)] * 2,
+        out_specs=[pl.BlockSpec(memory_space=pl.ANY)] * 2,
+        scratch_shapes=[v(2 * SYS, LN), v(2, 64, 64, 64), v(8, LN), v(2, ITERS + 1), sem(2 * CHUNKS), sem(2 * CHUNKS, 2), sem(2)],
         compiler_params=pltpu.CompilerParams(vmem_limit_bytes=60 * 1024 * 1024),
         name='unpack',
     )(xp, hist)

time: 184 us -> 177 us (0.962)
  Pallas kernels: 183 us -> 176 us
    pallas_call x1, Pallas kernels: 178 us -> 173 us  [run(): pl.pallas_call(kernel, out_shape=(jax.ShapeDtypeStruct((2 * SYS, LN), F32...]
where the time goes in v4:
time: 177 us
  Pallas kernels  176 us (99%)
    pallas_call x1, Pallas kernels, run(): pl.pallas_call(kernel, out_shape=(jax.ShapeDtypeStruct((2 * SYS, LN), F32...  173 us

profile of v4, /device:TPU:0, one launch (start us, length us, event | category | flops | bytes accessed | tf_op | source)
XLA Modules:
  0.0 176.7 jit_solution(17603255800804782606)
XLA Ops:
  0.6 172.7 %cg.1 = (f32[4096,128]{1,0:T(8,128)}, f32[8,128]{1,0:T(8,128)}) custom-call(f32[2,64,64,64]{3,2,1,0:T(8,128)} %s_hbm.1, f32[2,64,64,64]{3,2,1,0:T(8,128)} %b_hbm.1, f32[2,64,64,64]{3,2,1,0:T(8,128)} %x0_hbm.1, f32[2,64,64,64]{3,2,1,0:T(8,128)} %kx_hbm.1, f32[2,64,64,64]{3,2,1,0:T(8,128)} %ky_hbm.1, f32[2,64,64,64]{3,2,1,0:T(8,128)} %kz_hbm.1), custom_call_target="tpu_custom_call" | custom-call | tf_op jit(solution)/shard_map/cg/pallas_call | solution.py:438
  173.3 3.4 %unpack.1 = (f32[2,64,64,64]{3,2,1,0:T(8,128)}, f32[2,21]{1,0:T(2,128)}) custom-call(f32[4096,128]{1,0:T(8,128)} %get-tuple-element.4.xp, f32[8,128]{1,0:T(8,128)} %get-tuple-element.5.hist), custom_call_target="tpu_custom_call" | custom-call | tf_op jit(solution)/shard_map/unpack/pallas_call | solution.py:447

commit v5 on v4

--- a/solution.py
+++ b/solution.py
@@ -194,6 +194,21 @@
 
     def wide(vec, n):
         return jnp.broadcast_to(vec[None], (n // 8, 8, LN)).reshape(n, LN)
+
+    def z_face(ref, c):
+        def plane(x, T):
+            return pick(T, ref[rows(x, c)], x, zf)
+        sz[c] = lax.fori_loop(0, NP, plane, zero32, unroll=8)
+        sy[c] = ref[pl.ds(c * SYS + yf, 32, stride=NR)]
+
+    def turn_r(c):
+        G = rhz[c]
+        mask = face_mask(NR)
+
+        def plane(x, carry):
+            RZ[rows(x, c)] = jnp.where(mask, spread(G, x, zf), roll(R[rows(x, c)], to_z))
+            return carry
+        lax.fori_loop(0, NP, plane, 0, unroll=8)
 
     def r_copies(c):
         return [
@@ -242,33 +257,16 @@
             return acc + fold(r * r), fx, kxv, nxt
         acc, _, _, _ = lax.fori_loop(0, NP, start_plane, (jnp.zeros((8, LN), F32), KXM[c] * (low - u_first), KXM[c], u_first), unroll=4)
         reduce_start(0, c, acc)
-
-    def z_face(ref, c):
-        def plane(x, T):
-            return pick(T, ref[rows(x, c)], x, zf)
-        sz[c] = lax.fori_loop(0, NP, plane, zero32, unroll=8)
-        sy[c] = ref[pl.ds(c * SYS + yf, 32, stride=NR)]
-
-    def turn_r(c):
-        G = rhz[c]
-        mask = face_mask(NR)
-
-        def plane(x, carry):
-            RZ[rows(x, c)] = jnp.where(mask, spread(G, x, zf), roll(R[rows(x, c)], to_z))
-            return carry
-        lax.fori_loop(0, NP, plane, 0, unroll=8)
-
-    for c in range(2):
         z_face(R, c)
         for cp in r_copies(c):
             cp.start()
+
+    hist_s[...] = jnp.zeros((8, LN), F32)
+    for c in range(2):
         phx[c] = jnp.zeros((NR, LN), F32)
         phy[c] = zero32
-    hist_s[...] = jnp.zeros((8, LN), F32)
-    for c in range(2):
         for cp in r_copies(c):
-            cp.wait()
-        turn_r(c)
+            cp.wait_send()
 
     def q_copies(c, par):
         return [
@@ -330,11 +328,14 @@
             cur, kxp_prev = nxt, kxp
         return acc
 
-    CH = 512
-
     def body(k, carry):
         par = k % 2
         for c in range(2):
+            @pl.when(k == 0)
+            def _():
+                for cp in r_copies(c):
+                    cp.wait_recv()
+            turn_r(c)
             rho = reduce_end(0, c)
             note(c, k, rho)
             beta = jnp.where(k == 0, 0.0, rho / rho_s[c])
@@ -349,14 +350,13 @@
         for c in range(2):
             alpha = rho_s[c] / reduce_end(1, c)
             alpha_s[c] = alpha
-            a_ch = wide(alpha, CH)
-
-            def step_r(i, acc):
-                at = pl.ds(pl.multiple_of(c * SYS + i * CH, 8), CH)
+            a_ch = wide(alpha, NR)
+            acc = jnp.zeros((8, LN), F32)
+            for x in range(NP):
+                at = pl.ds(c * SYS + x * NR, NR)
                 r = R[at] - a_ch * Q[at]
                 R[at] = r
-                return acc + fold(r * r)
-            acc = lax.fori_loop(0, SYS // CH, step_r, jnp.zeros((8, LN), F32))
+                acc = acc + fold(r * r)
             reduce_start(0, c, acc)
 
             def step_x(x, carry):
@@ -372,7 +372,6 @@
             rhx[c] = rhx[c] - wide(alpha, NR) * qhx[par, c]
             rhy[c] = rhy[c] - wide(alpha, 32) * qhy[par, c]
             rhz[c] = rhz[c] - wide(alpha, 32) * qhz[par, c]
-            turn_r(c)
         return carry
 
     lax.fori_loop(0, ITERS, body, 0)

time: 177 us -> 176 us (level)
  no operation moved by 1% of the time
where the time goes in v5:
time: 176 us; the launch traced here: 175 us
  Pallas kernels  175 us (99%)
    pallas_call x1, Pallas kernels, run(): pl.pallas_call(kernel, out_shape=(jax.ShapeDtypeStruct((2 * SYS, LN), F32...  171 us

profile of v5, /device:TPU:0, one launch (start us, length us, event | category | flops | bytes accessed | tf_op | source)
XLA Modules:
  0.0 175.4 jit_solution(9346191567630913341)
XLA Ops:
  0.6 171.4 %cg.1 = (f32[4096,128]{1,0:T(8,128)}, f32[8,128]{1,0:T(8,128)}) custom-call(f32[2,64,64,64]{3,2,1,0:T(8,128)} %s_hbm.1, f32[2,64,64,64]{3,2,1,0:T(8,128)} %b_hbm.1, f32[2,64,64,64]{3,2,1,0:T(8,128)} %x0_hbm.1, f32[2,64,64,64]{3,2,1,0:T(8,128)} %kx_hbm.1, f32[2,64,64,64]{3,2,1,0:T(8,128)} %ky_hbm.1, f32[2,64,64,64]{3,2,1,0:T(8,128)} %kz_hbm.1), custom_call_target="tpu_custom_call" | custom-call | tf_op jit(solution)/shard_map/cg/pallas_call | solution.py:437
  172.1 3.4 %unpack.1 = (f32[2,64,64,64]{3,2,1,0:T(8,128)}, f32[2,21]{1,0:T(2,128)}) custom-call(f32[4096,128]{1,0:T(8,128)} %get-tuple-element.4.xp, f32[8,128]{1,0:T(8,128)} %get-tuple-element.5.hist), custom_call_target="tpu_custom_call" | custom-call | tf_op jit(solution)/shard_map/unpack/pallas_call | solution.py:446

commit v6 on v5

--- a/solution.py
+++ b/solution.py
@@ -328,6 +328,8 @@
             cur, kxp_prev = nxt, kxp
         return acc
 
+    outs = [pltpu.make_async_copy(X.at[pl.ds(c * SYS, SYS)], x_out.at[pl.ds(c * SYS, SYS)], out_sem.at[c]) for c in range(2)]
+
     def body(k, carry):
         par = k % 2
         for c in range(2):
@@ -335,15 +337,13 @@
             def _():
                 for cp in r_copies(c):
                     cp.wait_recv()
-            turn_r(c)
+                turn_r(c)
             rho = reduce_end(0, c)
             note(c, k, rho)
             beta = jnp.where(k == 0, 0.0, rho / rho_s[c])
             rho_s[c] = rho
             reduce_start(1, c, product(c, beta))
-        for c in range(2):
             reduce_sent(0, c)
-
             z_face(Q, c)
             for cp in q_copies(c, par):
                 cp.start()
@@ -364,20 +364,25 @@
                 X[at] = X[at] + wide(alpha, NR) * PB[pl.ds(pl.multiple_of(c * PSYS + x * PR + 8, 8), NR)]
                 return carry
             lax.fori_loop(0, NP, step_x, 0, unroll=4)
+
+            @pl.when(k == ITERS - 1)
+            def _():
+                outs[c].start()
         for c in range(2):
             reduce_sent(1, c)
             for cp in q_copies(c, par):
                 cp.wait()
-            alpha = alpha_s[c]
-            rhx[c] = rhx[c] - wide(alpha, NR) * qhx[par, c]
-            rhy[c] = rhy[c] - wide(alpha, 32) * qhy[par, c]
-            rhz[c] = rhz[c] - wide(alpha, 32) * qhz[par, c]
+
+            @pl.when(k < ITERS - 1)
+            def _():
+                alpha = alpha_s[c]
+                rhx[c] = rhx[c] - wide(alpha, NR) * qhx[par, c]
+                rhy[c] = rhy[c] - wide(alpha, 32) * qhy[par, c]
+                rhz[c] = rhz[c] - wide(alpha, 32) * qhz[par, c]
+                turn_r(c)
         return carry
 
     lax.fori_loop(0, ITERS, body, 0)
-    outs = [pltpu.make_async_copy(X.at[pl.ds(c * SYS, SYS)], x_out.at[pl.ds(c * SYS, SYS)], out_sem.at[c]) for c in range(2)]
-    for cp in outs:
-        cp.start()
     for c in range(2):
         note(c, ITERS, reduce_end(0, c))
         reduce_sent(0, c)

time: 176 us -> 179 us (1.017)
  Pallas kernels: 175 us -> 178 us
    pallas_call x1, Pallas kernels: 171 us -> 174 us  [run(): pl.pallas_call(kernel, out_shape=(jax.ShapeDtypeStruct((2 * SYS, LN), F32...]
where the time goes in v6:
time: 179 us; the launch traced here: 178 us
  Pallas kernels  178 us (99%)
    pallas_call x1, Pallas kernels, run(): pl.pallas_call(kernel, out_shape=(jax.ShapeDtypeStruct((2 * SYS, LN), F32...  174 us

profile of v6, /device:TPU:0, one launch (start us, length us, event | category | flops | bytes accessed | tf_op | source)
XLA Modules:
  0.0 178.4 jit_solution(6675087164774721180)
XLA Ops:
  0.6 174.4 %cg.1 = (f32[4096,128]{1,0:T(8,128)}, f32[8,128]{1,0:T(8,128)}) custom-call(f32[2,64,64,64]{3,2,1,0:T(8,128)} %s_hbm.1, f32[2,64,64,64]{3,2,1,0:T(8,128)} %b_hbm.1, f32[2,64,64,64]{3,2,1,0:T(8,128)} %x0_hbm.1, f32[2,64,64,64]{3,2,1,0:T(8,128)} %kx_hbm.1, f32[2,64,64,64]{3,2,1,0:T(8,128)} %ky_hbm.1, f32[2,64,64,64]{3,2,1,0:T(8,128)} %kz_hbm.1), custom_call_target="tpu_custom_call" | custom-call | tf_op jit(solution)/shard_map/cg/pallas_call | solution.py:442
  175.1 3.4 %unpack.1 = (f32[2,64,64,64]{3,2,1,0:T(8,128)}, f32[2,21]{1,0:T(2,128)}) custom-call(f32[4096,128]{1,0:T(8,128)} %get-tuple-element.4.xp, f32[8,128]{1,0:T(8,128)} %get-tuple-element.5.hist), custom_call_target="tpu_custom_call" | custom-call | tf_op jit(solution)/shard_map/unpack/pallas_call | solution.py:451

commit v7 on v5

--- a/solution.py
+++ b/solution.py
@@ -267,6 +267,9 @@
         phy[c] = zero32
         for cp in r_copies(c):
             cp.wait_send()
+    for cp in r_copies(0):
+        cp.wait_recv()
+    turn_r(0)
 
     def q_copies(c, par):
         return [
@@ -328,59 +331,81 @@
             cur, kxp_prev = nxt, kxp
         return acc
 
+    outs = [pltpu.make_async_copy(X.at[pl.ds(c * SYS, SYS)], x_out.at[pl.ds(c * SYS, SYS)], out_sem.at[c]) for c in range(2)]
+
+    def halo_r(c, par):
+        for cp in q_copies(c, par):
+            cp.wait_recv()
+        alpha = alpha_s[c]
+        rhx[c] = rhx[c] - wide(alpha, NR) * qhx[par, c]
+        rhy[c] = rhy[c] - wide(alpha, 32) * qhy[par, c]
+        rhz[c] = rhz[c] - wide(alpha, 32) * qhz[par, c]
+
+    def q_sent(c, par):
+        for cp in q_copies(c, par):
+            cp.wait_send()
+
+    def first_half(c, k, par):
+        rho = reduce_end(0, c)
+        note(c, k, rho)
+        beta = jnp.where(k == 0, 0.0, rho / rho_s[c])
+        rho_s[c] = rho
+        reduce_start(1, c, product(c, beta))
+        reduce_sent(0, c)
+        z_face(Q, c)
+        for cp in q_copies(c, par):
+            cp.start()
+
+    def second_half(c, k):
+        alpha = rho_s[c] / reduce_end(1, c)
+        alpha_s[c] = alpha
+        a_pl = wide(alpha, NR)
+        acc = jnp.zeros((8, LN), F32)
+        for x in range(NP):
+            at = pl.ds(c * SYS + x * NR, NR)
+            r = R[at] - a_pl * Q[at]
+            R[at] = r
+            acc = acc + fold(r * r)
+        reduce_start(0, c, acc)
+
+        def step_x(x, carry):
+            X[rows(x, c)] = X[rows(x, c)] + a_pl * PB[pl.ds(pl.multiple_of(c * PSYS + x * PR + 8, 8), NR)]
+            return carry
+        lax.fori_loop(0, NP, step_x, 0, unroll=4)
+
+        @pl.when(k == ITERS - 1)
+        def _():
+            outs[c].start()
+        reduce_sent(1, c)
+
     def body(k, carry):
         par = k % 2
-        for c in range(2):
-            @pl.when(k == 0)
-            def _():
-                for cp in r_copies(c):
-                    cp.wait_recv()
-            turn_r(c)
-            rho = reduce_end(0, c)
-            note(c, k, rho)
-            beta = jnp.where(k == 0, 0.0, rho / rho_s[c])
-            rho_s[c] = rho
-            reduce_start(1, c, product(c, beta))
-        for c in range(2):
-            reduce_sent(0, c)
-
-            z_face(Q, c)
-            for cp in q_copies(c, par):
-                cp.start()
-        for c in range(2):
-            alpha = rho_s[c] / reduce_end(1, c)
-            alpha_s[c] = alpha
-            a_ch = wide(alpha, NR)
-            acc = jnp.zeros((8, LN), F32)
-            for x in range(NP):
-                at = pl.ds(c * SYS + x * NR, NR)
-                r = R[at] - a_ch * Q[at]
-                R[at] = r
-                acc = acc + fold(r * r)
-            reduce_start(0, c, acc)
-
-            def step_x(x, carry):
-                at = pl.ds(pl.multiple_of(c * SYS + x * NR, 8), NR)
-                X[at] = X[at] + wide(alpha, NR) * PB[pl.ds(pl.multiple_of(c * PSYS + x * PR + 8, 8), NR)]
-                return carry
-            lax.fori_loop(0, NP, step_x, 0, unroll=4)
-        for c in range(2):
-            reduce_sent(1, c)
-            for cp in q_copies(c, par):
-                cp.wait()
-            alpha = alpha_s[c]
-            rhx[c] = rhx[c] - wide(alpha, NR) * qhx[par, c]
-            rhy[c] = rhy[c] - wide(alpha, 32) * qhy[par, c]
-            rhz[c] = rhz[c] - wide(alpha, 32) * qhz[par, c]
+        first_half(0, k, par)
+
+        @pl.when(k == 0)
+        def _():
+            for cp in r_copies(1):
+                cp.wait_recv()
+
+        @pl.when(k > 0)
+        def _():
+            halo_r(1, 1 - par)
+            q_sent(1, 1 - par)
+        turn_r(1)
+        first_half(1, k, par)
+        second_half(0, k)
+        halo_r(0, par)
+        turn_r(0)
+        second_half(1, k)
+        q_sent(0, par)
         return carry
 
     lax.fori_loop(0, ITERS, body, 0)
-    outs = [pltpu.make_async_copy(X.at[pl.ds(c * SYS, SYS)], x_out.at[pl.ds(c * SYS, SYS)], out_sem.at[c]) for c in range(2)]
-    for cp in outs:
-        cp.start()
     for c in range(2):
         note(c, ITERS, reduce_end(0, c))
         reduce_sent(0, c)
+    for cp in q_copies(1, (ITERS - 1) % 2):
+        cp.wait()
     hist_out[...] = jnp.sqrt(hist_s[...] * (1.0 / (128 * 128 * 128)))
     for cp in outs:
         cp.wait()

time: 176 us -> 173 us (0.983)
  Pallas kernels: 175 us -> 173 us
    pallas_call x1, Pallas kernels: 171 us -> 169 us  [run(): pl.pallas_call(kernel, out_shape=(jax.ShapeDtypeStruct((2 * SYS, LN), F32...]
where the time goes in v7:
time: 173 us
  Pallas kernels  173 us (100%)
    pallas_call x1, Pallas kernels, run(): pl.pallas_call(kernel, out_shape=(jax.ShapeDtypeStruct((2 * SYS, LN), F32...  169 us

profile of v7, /device:TPU:0, one launch (start us, length us, event | category | flops | bytes accessed | tf_op | source)
XLA Modules:
  0.0 173.4 jit_solution(1017436535569090878)
XLA Ops:
  0.6 169.3 %cg.1 = (f32[4096,128]{1,0:T(8,128)}, f32[8,128]{1,0:T(8,128)}) custom-call(f32[2,64,64,64]{3,2,1,0:T(8,128)} %s_hbm.1, f32[2,64,64,64]{3,2,1,0:T(8,128)} %b_hbm.1, f32[2,64,64,64]{3,2,1,0:T(8,128)} %x0_hbm.1, f32[2,64,64,64]{3,2,1,0:T(8,128)} %kx_hbm.1, f32[2,64,64,64]{3,2,1,0:T(8,128)} %ky_hbm.1, f32[2,64,64,64]{3,2,1,0:T(8,128)} %kz_hbm.1), custom_call_target="tpu_custom_call" | custom-call | tf_op jit(solution)/shard_map/cg/pallas_call | solution.py:462
  170.0 3.4 %unpack.1 = (f32[2,64,64,64]{3,2,1,0:T(8,128)}, f32[2,21]{1,0:T(2,128)}) custom-call(f32[4096,128]{1,0:T(8,128)} %get-tuple-element.4.xp, f32[8,128]{1,0:T(8,128)} %get-tuple-element.5.hist), custom_call_target="tpu_custom_call" | custom-call | tf_op jit(solution)/shard_map/unpack/pallas_call | solution.py:471

commit v8 on v7

--- a/solution.py
+++ b/solution.py
@@ -17,6 +17,7 @@
 SYS = NP * NR
 PSYS = (NP + 1) * PR
 KSYS = NP * KR
+IN_FLIGHT = 3
 AHEAD = 3
 
 
@@ -29,7 +30,7 @@
 def kernel(s_hbm, b_hbm, x0_hbm, kx_hbm, ky_hbm, kz_hbm, x_out, hist_out,
            st_s, st_b, st_x, st_kx, st_ky, st_kz,
            X, R, Q, PB, PZ, RZ, KX, KXM, KY, KZ, KZF, D, KF,
-           ix, iy, iz, jx, jy, jz, sxy, sxz, sky, skz, sy, sz,
+           ix, iy, iz, jx, jy, jz, sxy, sxz, sky, skz, sy, sz, sry, srz,
            rhx, rhy, rhz, phx, phy, qhx, qhy, qhz,
            red, rho_s, alpha_s, hist_s,
            ld_sem, isend, irecv, rsend, rrecv, qsend, qrecv, dsend, drecv, out_sem):
@@ -58,13 +59,17 @@
     def splits(n):
         return lanes(n) < 64
 
-    loads = []
-    for num, (src, dst) in enumerate(((x0_hbm, st_x), (kz_hbm, st_kz), (kx_hbm, st_kx), (ky_hbm, st_ky), (s_hbm, st_s), (b_hbm, st_b))):
-        pair = [pltpu.make_async_copy(src.at[c], dst.at[c], ld_sem.at[num, c]) for c in range(2)]
-        loads.append(pair)
-    for num in range(1):
-        for cp in loads[num]:
-            cp.start()
+    order = [(num, c) for c in range(2) for num in range(6)]
+    pairs = ((x0_hbm, st_x), (kz_hbm, st_kz), (ky_hbm, st_ky), (kx_hbm, st_kx), (s_hbm, st_s), (b_hbm, st_b))
+    loads = [pltpu.make_async_copy(pairs[num][0].at[c], pairs[num][1].at[c], ld_sem.at[num, c]) for num, c in order]
+    for cp in loads[:IN_FLIGHT]:
+        cp.start()
+
+    def loaded(num, c):
+        n = c * 6 + num
+        loads[n].wait()
+        if n + IN_FLIGHT < len(loads):
+            loads[n + IN_FLIGHT].start()
 
     barrier = pltpu.get_barrier_semaphore()
     for m in range(1, 8):
@@ -102,11 +107,8 @@
             remote(sky.at[c], jy.at[c], isend.at[c, 4], irecv.at[c, 4], nbr['y']),
             remote(KX.at[pl.ds(c * SYS + 31 * NR, NR)], jx.at[c], isend.at[c, 5], irecv.at[c, 5], nbr['x'])])
 
-    for c in range(2):
-        loads[0][c].wait()
-        for num in ((1, 2), (3, 4, 5))[c]:
-            for cp in loads[num]:
-                cp.start()
+    def prepare_x0(c):
+        loaded(0, c)
 
         def pack_x(x, T):
             u = packed(st_x, c, x)
@@ -118,12 +120,9 @@
             return pick(T, u, x, zf)
         sxz[c] = lax.fori_loop(0, NP, pack_x, zero32, unroll=8)
         sxy[c] = X[pl.ds(c * SYS + yf, 32, stride=NR)]
-    pl.semaphore_wait(barrier, 7)
-    for c in range(2):
-        for cp in first[c][:3]:
-            cp.start()
-    for c in range(2):
-        loads[1][c].wait()
+
+    def prepare_kz(c):
+        loaded(1, c)
 
         def pack_z(x, T):
             u = packed(st_kz, c, x)
@@ -133,19 +132,9 @@
             KZF[rows(x, c)] = jnp.where(pz == 1, inner, moved)
             return pick(T, u, x, 63)
         skz[c] = lax.fori_loop(0, NP, pack_z, zero32, unroll=8)
-    for c in range(2):
-        loads[2][c].wait()
-
-        def pack_kx(x, carry):
-            KX[rows(x, c)] = packed(st_kx, c, x)
-            return carry
-        lax.fori_loop(0, NP, pack_kx, 0, unroll=8)
-        last = KX[pl.ds(c * SYS + 31 * NR, NR)]
-        edge = jnp.logical_and(lanes(NR) >= 64, px == 1)
-        KX[pl.ds(c * SYS + 31 * NR, NR)] = jnp.where(edge, 0.0, last)
-        first[c][3].start()
-    for c in range(2):
-        loads[3][c].wait()
+
+    def prepare_ky(c):
+        loaded(2, c)
 
         def pack_ky(x, carry):
             u = packed(st_ky, c, x)
@@ -155,19 +144,46 @@
             return carry
         lax.fori_loop(0, NP, pack_ky, 0, unroll=8)
         sky[c] = KY[pl.ds(c * KSYS + 71, 32, stride=KR)]
-        first[c][5].start()
-    for c in range(2):
-        loads[4][c].wait()
-        loads[5][c].wait()
-        if c == 0:
-            for cp in (first[0][4], first[1][4]):
-                cp.start()
+
+    def prepare_kx(c):
+        loaded(3, c)
+
+        def pack_kx(x, carry):
+            KX[rows(x, c)] = packed(st_kx, c, x)
+            return carry
+        lax.fori_loop(0, NP, pack_kx, 0, unroll=8)
+        last = KX[pl.ds(c * SYS + 31 * NR, NR)]
+        edge = jnp.logical_and(lanes(NR) >= 64, px == 1)
+        KX[pl.ds(c * SYS + 31 * NR, NR)] = jnp.where(edge, 0.0, last)
+
+    def prepare_sb(c):
+        loaded(4, c)
+        loaded(5, c)
 
         def pack_sb(x, carry):
             D[rows(x, c)] = packed(st_s, c, x)
             R[rows(x, c)] = packed(st_b, c, x)
             return carry
         lax.fori_loop(0, NP, pack_sb, 0, unroll=8)
+
+    prepare_x0(0)
+    pl.semaphore_wait(barrier, 7)
+    for cp in first[0][:3]:
+        cp.start()
+    prepare_kz(0)
+    first[0][3].start()
+    prepare_ky(0)
+    first[0][4].start()
+    prepare_kx(0)
+    first[0][5].start()
+    prepare_sb(0)
+    prepare_x0(1)
+    for cp in first[1][:3]:
+        cp.start()
+    prepare_kz(1)
+    first[1][3].start()
+    prepare_ky(1)
+    first[1][4].start()
 
     def reduce_copies(kind, c):
         return [remote(red.at[kind, c, 0], red.at[kind, c, m], dsend.at[kind, c, m], drecv.at[kind, c, m], others[m]) for m in (7, 6, 5, 4, 3, 2, 1)]
@@ -195,11 +211,11 @@
     def wide(vec, n):
         return jnp.broadcast_to(vec[None], (n // 8, 8, LN)).reshape(n, LN)
 
-    def z_face(ref, c):
+    def z_face(ref, c, to_sz, to_sy):
         def plane(x, T):
             return pick(T, ref[rows(x, c)], x, zf)
-        sz[c] = lax.fori_loop(0, NP, plane, zero32, unroll=8)
-        sy[c] = ref[pl.ds(c * SYS + yf, 32, stride=NR)]
+        to_sz[c] = lax.fori_loop(0, NP, plane, zero32, unroll=8)
+        to_sy[c] = ref[pl.ds(c * SYS + yf, 32, stride=NR)]
 
     def turn_r(c):
         G = rhz[c]
@@ -212,13 +228,13 @@
 
     def r_copies(c):
         return [
-            remote(sz.at[c], rhz.at[c], rsend.at[c, 0], rrecv.at[c, 0], nbr['z']),
-            remote(sy.at[c], rhy.at[c], rsend.at[c, 1], rrecv.at[c, 1], nbr['y']),
+            remote(srz.at[c], rhz.at[c], rsend.at[c, 0], rrecv.at[c, 0], nbr['z']),
+            remote(sry.at[c], rhy.at[c], rsend.at[c, 1], rrecv.at[c, 1], nbr['y']),
             remote(x_plane(R, c), rhx.at[c], rsend.at[c, 2], rrecv.at[c, 2], nbr['x'])]
 
-    for c in range(2):
+    def start(c):
         for cp in first[c]:
-            cp.wait()
+            cp.wait_recv()
         lo = splits(NR)
         kx_last = KX[pl.ds(c * SYS + 31 * NR, NR)]
         KXM[c] = roll(jnp.where(lo, kx_last, jnp.where(px == 1, jx[c], 0.0)), 64)
@@ -255,17 +271,23 @@
             r = R[at] - (s * u + (fx - fx_prev) + (kyv * (u - yu) - kyl * (yl - u)) + (fz - fz_away))
             R[at] = r
             return acc + fold(r * r), fx, kxv, nxt
-        acc, _, _, _ = lax.fori_loop(0, NP, start_plane, (jnp.zeros((8, LN), F32), KXM[c] * (low - u_first), KXM[c], u_first), unroll=4)
+        init = (jnp.zeros((8, LN), F32), KXM[c] * (low - u_first), KXM[c], u_first)
+        acc = lax.fori_loop(0, NP, start_plane, init, unroll=4)[0]
         reduce_start(0, c, acc)
-        z_face(R, c)
+        z_face(R, c, srz, sry)
         for cp in r_copies(c):
             cp.start()
 
+    start(0)
+    prepare_kx(1)
+    first[1][5].start()
+    prepare_sb(1)
+    start(1)
     hist_s[...] = jnp.zeros((8, LN), F32)
     for c in range(2):
         phx[c] = jnp.zeros((NR, LN), F32)
         phy[c] = zero32
-        for cp in r_copies(c):
+        for cp in first[c]:
             cp.wait_send()
     for cp in r_copies(0):
         cp.wait_recv()
@@ -352,7 +374,7 @@
         rho_s[c] = rho
         reduce_start(1, c, product(c, beta))
         reduce_sent(0, c)
-        z_face(Q, c)
+        z_face(Q, c, sz, sy)
         for cp in q_copies(c, par):
             cp.start()
 
@@ -393,6 +415,12 @@
             q_sent(1, 1 - par)
         turn_r(1)
         first_half(1, k, par)
+
+        @pl.when(k == 0)
+        def _():
+            for c in range(2):
+                for cp in r_copies(c):
+                    cp.wait_send()
         second_half(0, k)
         halo_r(0, par)
         turn_r(0)
@@ -454,7 +482,7 @@
     full = v(2 * SYS, LN)
     scratch += [full, full, full, v(2 * PSYS, LN), full, full, full, v(2, NR, LN), v(2 * KSYS, LN), full, full, full, v(2, 32, LN)]
     scratch += [v(2, NR, LN), v(2, 32, LN), v(2, 32, LN)] * 2
-    scratch += [v(2, 32, LN)] * 6
+    scratch += [v(2, 32, LN)] * 8
     scratch += [v(2, NR, LN), v(2, 32, LN), v(2, 32, LN), v(2, NR, LN), v(2, 32, LN)]
     scratch += [v(2, 2, NR, LN), v(2, 2, 32, LN), v(2, 2, 32, LN)]
     scratch += [v(2, 2, 8, 1, LN), v(2, 8, LN), v(2, 8, LN), v(8, LN)]

time: 173 us -> 172 us (level)
  Pallas kernels: 173 us -> 171 us
where the time goes in v8:
time: 172 us
  Pallas kernels  171 us (99%)
    pallas_call x1, Pallas kernels, run(): pl.pallas_call(kernel, out_shape=(jax.ShapeDtypeStruct((2 * SYS, LN), F32...  168 us

profile of v8, /device:TPU:0, one launch (start us, length us, event | category | flops | bytes accessed | tf_op | source)
XLA Modules:
  0.0 171.7 jit_solution(16060328455862702726)
XLA Ops:
  0.6 167.7 %cg.1 = (f32[4096,128]{1,0:T(8,128)}, f32[8,128]{1,0:T(8,128)}) custom-call(f32[2,64,64,64]{3,2,1,0:T(8,128)} %s_hbm.1, f32[2,64,64,64]{3,2,1,0:T(8,128)} %b_hbm.1, f32[2,64,64,64]{3,2,1,0:T(8,128)} %x0_hbm.1, f32[2,64,64,64]{3,2,1,0:T(8,128)} %kx_hbm.1, f32[2,64,64,64]{3,2,1,0:T(8,128)} %ky_hbm.1, f32[2,64,64,64]{3,2,1,0:T(8,128)} %kz_hbm.1), custom_call_target="tpu_custom_call" | custom-call | tf_op jit(solution)/shard_map/cg/pallas_call | solution.py:490
  168.3 3.4 %unpack.1 = (f32[2,64,64,64]{3,2,1,0:T(8,128)}, f32[2,21]{1,0:T(2,128)}) custom-call(f32[4096,128]{1,0:T(8,128)} %get-tuple-element.4.xp, f32[8,128]{1,0:T(8,128)} %get-tuple-element.5.hist), custom_call_target="tpu_custom_call" | custom-call | tf_op jit(solution)/shard_map/unpack/pallas_call | solution.py:499

commit v9 on v8

--- a/solution.py
+++ b/solution.py
@@ -422,9 +422,9 @@
                 for cp in r_copies(c):
                     cp.wait_send()
         second_half(0, k)
+        second_half(1, k)
         halo_r(0, par)
         turn_r(0)
-        second_half(1, k)
         q_sent(0, par)
         return carry
 

time: 172 us -> 176 us (1.023)
  Pallas kernels: 171 us -> 176 us
    pallas_call x1, Pallas kernels: 168 us -> 172 us  [run(): pl.pallas_call(kernel, out_shape=(jax.ShapeDtypeStruct((2 * SYS, LN), F32...]
where the time goes in v9:
time: 176 us
  Pallas kernels  176 us (100%)
    pallas_call x1, Pallas kernels, run(): pl.pallas_call(kernel, out_shape=(jax.ShapeDtypeStruct((2 * SYS, LN), F32...  172 us

profile of v9, /device:TPU:0, one launch (start us, length us, event | category | flops | bytes accessed | tf_op | source)
XLA Modules:
  0.0 176.3 jit_solution(2654463100875293834)
XLA Ops:
  0.6 172.3 %cg.1 = (f32[4096,128]{1,0:T(8,128)}, f32[8,128]{1,0:T(8,128)}) custom-call(f32[2,64,64,64]{3,2,1,0:T(8,128)} %s_hbm.1, f32[2,64,64,64]{3,2,1,0:T(8,128)} %b_hbm.1, f32[2,64,64,64]{3,2,1,0:T(8,128)} %x0_hbm.1, f32[2,64,64,64]{3,2,1,0:T(8,128)} %kx_hbm.1, f32[2,64,64,64]{3,2,1,0:T(8,128)} %ky_hbm.1, f32[2,64,64,64]{3,2,1,0:T(8,128)} %kz_hbm.1), custom_call_target="tpu_custom_call" | custom-call | tf_op jit(solution)/shard_map/cg/pallas_call | solution.py:490
  173.0 3.4 %unpack.1 = (f32[2,64,64,64]{3,2,1,0:T(8,128)}, f32[2,21]{1,0:T(2,128)}) custom-call(f32[4096,128]{1,0:T(8,128)} %get-tuple-element.4.xp, f32[8,128]{1,0:T(8,128)} %get-tuple-element.5.hist), custom_call_target="tpu_custom_call" | custom-call | tf_op jit(solution)/shard_map/unpack/pallas_call | solution.py:499

commit v10 on v8

--- a/solution.py
+++ b/solution.py
@@ -193,9 +193,11 @@
         for cp in reduce_copies(kind, c):
             cp.start()
 
-    def reduce_end(kind, c):
+    def reduce_arrived(kind, c):
         for cp in reduce_copies(kind, c):
             cp.wait_recv()
+
+    def reduce_end(kind, c):
         v = [red[kind, c, m] for m in range(8)]
         total = ((v[0] + v[1]) + (v[2] + v[3])) + ((v[4] + v[5]) + (v[6] + v[7]))
         total = jnp.broadcast_to(total, (8, LN))
@@ -292,6 +294,7 @@
     for cp in r_copies(0):
         cp.wait_recv()
     turn_r(0)
+    reduce_arrived(0, 1)
 
     def q_copies(c, par):
         return [
@@ -368,6 +371,10 @@
             cp.wait_send()
 
     def first_half(c, k, par):
+        if c == 0:
+            reduce_arrived(0, c)
+        else:
+            pl.when(k > 0)(lambda: reduce_arrived(0, c))
         rho = reduce_end(0, c)
         note(c, k, rho)
         beta = jnp.where(k == 0, 0.0, rho / rho_s[c])
@@ -379,6 +386,7 @@
             cp.start()
 
     def second_half(c, k):
+        reduce_arrived(1, c)
         alpha = rho_s[c] / reduce_end(1, c)
         alpha_s[c] = alpha
         a_pl = wide(alpha, NR)
@@ -430,6 +438,7 @@
 
     lax.fori_loop(0, ITERS, body, 0)
     for c in range(2):
+        reduce_arrived(0, c)
         note(c, ITERS, reduce_end(0, c))
         reduce_sent(0, c)
     for cp in q_copies(1, (ITERS - 1) % 2):

time: 172 us -> 173 us (level)
  Pallas kernels: 171 us -> 173 us
where the time goes in v10:
time: 173 us
  Pallas kernels  173 us (100%)
    pallas_call x1, Pallas kernels, run(): pl.pallas_call(kernel, out_shape=(jax.ShapeDtypeStruct((2 * SYS, LN), F32...  169 us

profile of v10, /device:TPU:0, one launch (start us, length us, event | category | flops | bytes accessed | tf_op | source)
XLA Modules:
  0.0 173.4 jit_solution(14111807983025091970)
XLA Ops:
  0.6 169.4 %cg.1 = (f32[4096,128]{1,0:T(8,128)}, f32[8,128]{1,0:T(8,128)}) custom-call(f32[2,64,64,64]{3,2,1,0:T(8,128)} %s_hbm.1, f32[2,64,64,64]{3,2,1,0:T(8,128)} %b_hbm.1, f32[2,64,64,64]{3,2,1,0:T(8,128)} %x0_hbm.1, f32[2,64,64,64]{3,2,1,0:T(8,128)} %kx_hbm.1, f32[2,64,64,64]{3,2,1,0:T(8,128)} %ky_hbm.1, f32[2,64,64,64]{3,2,1,0:T(8,128)} %kz_hbm.1), custom_call_target="tpu_custom_call" | custom-call | tf_op jit(solution)/shard_map/cg/pallas_call | solution.py:499
  170.0 3.4 %unpack.1 = (f32[2,64,64,64]{3,2,1,0:T(8,128)}, f32[2,21]{1,0:T(2,128)}) custom-call(f32[4096,128]{1,0:T(8,128)} %get-tuple-element.4.xp, f32[8,128]{1,0:T(8,128)} %get-tuple-element.5.hist), custom_call_target="tpu_custom_call" | custom-call | tf_op jit(solution)/shard_map/unpack/pallas_call | solution.py:508

commit v11 on v8

--- a/solution.py
+++ b/solution.py
@@ -29,7 +29,7 @@
 
 def kernel(s_hbm, b_hbm, x0_hbm, kx_hbm, ky_hbm, kz_hbm, x_out, hist_out,
            st_s, st_b, st_x, st_kx, st_ky, st_kz,
-           X, R, Q, PB, PZ, RZ, KX, KXM, KY, KZ, KZF, D, KF,
+           X, R, Q, PB, PZ, RZ, KX, KXM, KY, KYL, KZ, KZF, D, KF,
            ix, iy, iz, jx, jy, jz, sxy, sxz, sky, skz, sy, sz, sry, srz,
            rhx, rhy, rhz, phx, phy, qhx, qhy, qhz,
            red, rho_s, alpha_s, hist_s,
@@ -267,6 +267,7 @@
             fz_away = roll(jnp.where(mask, 0.0, fz), fro_z)
             D[at] = s + (kxv + kx_prev) + (kyv + kyl) + (kzf + KZF[at])
             KZF[at] = kzf
+            KYL[at] = kyl
             PZ[at] = uz
             r = R[at] - (s * u + (fx - fx_prev) + (kyv * (u - yu) - kyl * (yl - u)) + (fz - fz_away))
             R[at] = r
@@ -344,7 +345,7 @@
             kxp = kxv * cur
             q = D[at] * cur - kxp_prev - kxv * nxt
             q = q - KY[pl.ds(kbase + 8, NR)] * PB[pl.ds(base + 9, NR)]
-            q = q - KY[pl.ds(kbase + 7, NR)] * PB[pl.ds(base + 7, NR)]
+            q = q - KYL[at] * PB[pl.ds(base + 7, NR)]
             pz_new = RZ[at] + b64 * PZ[at]
             PZ[at] = pz_new
             q = q - KZF[at] * pz_new - turned.pop(x)
@@ -480,7 +481,7 @@
     sem = lambda *shape: pltpu.SemaphoreType.DMA(shape)
     scratch = [v(2, 64, 64, 64)] * 6
     full = v(2 * SYS, LN)
-    scratch += [full, full, full, v(2 * PSYS, LN), full, full, full, v(2, NR, LN), v(2 * KSYS, LN), full, full, full, v(2, 32, LN)]
+    scratch += [full, full, full, v(2 * PSYS, LN), full, full, full, v(2, NR, LN), v(2 * KSYS, LN), full, full, full, full, v(2, 32, LN)]
     scratch += [v(2, NR, LN), v(2, 32, LN), v(2, 32, LN)] * 2
     scratch += [v(2, 32, LN)] * 8
     scratch += [v(2, NR, LN), v(2, 32, LN), v(2, 32, LN), v(2, NR, LN), v(2, 32, LN)]

time: 172 us -> 172 us (level)
  no operation moved by 1% of the time
where the time goes in v11:
time: 172 us
  Pallas kernels  171 us (99%)
    pallas_call x1, Pallas kernels, run(): pl.pallas_call(kernel, out_shape=(jax.ShapeDtypeStruct((2 * SYS, LN), F32...  168 us

profile of v11, /device:TPU:0, one launch (start us, length us, event | category | flops | bytes accessed | tf_op | source)
XLA Modules:
  0.0 171.7 jit_solution(3954257280820839655)
XLA Ops:
  0.6 167.7 %cg.1 = (f32[4096,128]{1,0:T(8,128)}, f32[8,128]{1,0:T(8,128)}) custom-call(f32[2,64,64,64]{3,2,1,0:T(8,128)} %s_hbm.1, f32[2,64,64,64]{3,2,1,0:T(8,128)} %b_hbm.1, f32[2,64,64,64]{3,2,1,0:T(8,128)} %x0_hbm.1, f32[2,64,64,64]{3,2,1,0:T(8,128)} %kx_hbm.1, f32[2,64,64,64]{3,2,1,0:T(8,128)} %ky_hbm.1, f32[2,64,64,64]{3,2,1,0:T(8,128)} %kz_hbm.1), custom_call_target="tpu_custom_call" | custom-call | tf_op jit(solution)/shard_map/cg/pallas_call | solution.py:491
  168.3 3.4 %unpack.1 = (f32[2,64,64,64]{3,2,1,0:T(8,128)}, f32[2,21]{1,0:T(2,128)}) custom-call(f32[4096,128]{1,0:T(8,128)} %get-tuple-element.4.xp, f32[8,128]{1,0:T(8,128)} %get-tuple-element.5.hist), custom_call_target="tpu_custom_call" | custom-call | tf_op jit(solution)/shard_map/unpack/pallas_call | solution.py:500

commit v12 on v8

--- a/solution.py
+++ b/solution.py
@@ -27,13 +27,13 @@
     return pltpu.roll(val, shift, 1)
 
 
-def kernel(s_hbm, b_hbm, x0_hbm, kx_hbm, ky_hbm, kz_hbm, x_out, hist_out,
+def kernel(s_hbm, b_hbm, x0_hbm, kx_hbm, ky_hbm, kz_hbm, X, hist_out,
            st_s, st_b, st_x, st_kx, st_ky, st_kz,
-           X, R, Q, PB, PZ, RZ, KX, KXM, KY, KZ, KZF, D, KF,
+           R, Q, PB, PZ, RZ, KX, KXM, KY, KZ, KZF, D, KF,
            ix, iy, iz, jx, jy, jz, sxy, sxz, sky, skz, sy, sz, sry, srz,
            rhx, rhy, rhz, phx, phy, qhx, qhy, qhz,
            red, rho_s, alpha_s, hist_s,
-           ld_sem, isend, irecv, rsend, rrecv, qsend, qrecv, dsend, drecv, out_sem):
+           ld_sem, isend, irecv, rsend, rrecv, qsend, qrecv, dsend, drecv):
     pz, py, px = lax.axis_index('pz'), lax.axis_index('py'), lax.axis_index('px')
     nbr = {'x': (pz, py, 1 - px), 'y': (pz, 1 - py, px), 'z': (1 - pz, py, px)}
     others = {}
@@ -353,8 +353,6 @@
             cur, kxp_prev = nxt, kxp
         return acc
 
-    outs = [pltpu.make_async_copy(X.at[pl.ds(c * SYS, SYS)], x_out.at[pl.ds(c * SYS, SYS)], out_sem.at[c]) for c in range(2)]
-
     def halo_r(c, par):
         for cp in q_copies(c, par):
             cp.wait_recv()
@@ -394,10 +392,6 @@
             X[rows(x, c)] = X[rows(x, c)] + a_pl * PB[pl.ds(pl.multiple_of(c * PSYS + x * PR + 8, 8), NR)]
             return carry
         lax.fori_loop(0, NP, step_x, 0, unroll=4)
-
-        @pl.when(k == ITERS - 1)
-        def _():
-            outs[c].start()
         reduce_sent(1, c)
 
     def body(k, carry):
@@ -435,42 +429,30 @@
     for cp in q_copies(1, (ITERS - 1) % 2):
         cp.wait()
     hist_out[...] = jnp.sqrt(hist_s[...] * (1.0 / (128 * 128 * 128)))
-    for cp in outs:
-        cp.wait()
-
-
-CHUNKS = 2
-VMEM_MAIN = 60 * 1024 * 1024
-
-
-def unpack(xp, hist, x_out, hist_out, buf, st, hs, ho, in_sem, out_sem, h_sem):
+
+
+CHUNKS = 4
+VMEM_MAIN = 54 * 1024 * 1024
+
+
+def unpack(buf, hist, x_out, hist_out, st, ho, out_sem, h_sem):
     planes = NP // CHUNKS
-    hist_in = pltpu.make_async_copy(hist, hs, h_sem.at[0])
-    hist_in.start()
-    loads = []
-    for n in range(2 * CHUNKS):
-        at = pl.ds(n * planes * NR, planes * NR)
-        loads.append(pltpu.make_async_copy(xp.at[at], buf.at[at], in_sem.at[n]))
-        loads[n].start()
-    stores = []
+    ho[...] = hist[:2, :ITERS + 1]
+    stores = [pltpu.make_async_copy(ho, hist_out, h_sem)]
+    stores[0].start()
     for n in range(2 * CHUNKS):
         c, x0 = n // CHUNKS, n % CHUNKS * planes
-        loads[n].wait()
 
         def plane(x, carry):
             val = buf[pl.ds(pl.multiple_of(n * planes * NR + x * NR, 8), NR)]
             st[c, x0 + x] = val[:, :64]
             st[c, x0 + x + NP] = roll(val, 64)[:, :64]
             return carry
-        lax.fori_loop(0, planes, plane, 0, unroll=16)
+        lax.fori_loop(0, planes, plane, 0, unroll=8)
         for h in range(2):
             at = pl.ds(x0 + NP * h, planes)
             stores.append(pltpu.make_async_copy(st.at[c, at], x_out.at[c, at], out_sem.at[n, h]))
             stores[-1].start()
-    hist_in.wait()
-    ho[...] = hs[:2, :ITERS + 1]
-    stores.append(pltpu.make_async_copy(ho, hist_out, h_sem.at[1]))
-    stores[-1].start()
     for cp in stores:
         cp.wait()
 
@@ -480,18 +462,18 @@
     sem = lambda *shape: pltpu.SemaphoreType.DMA(shape)
     scratch = [v(2, 64, 64, 64)] * 6
     full = v(2 * SYS, LN)
-    scratch += [full, full, full, v(2 * PSYS, LN), full, full, full, v(2, NR, LN), v(2 * KSYS, LN), full, full, full, v(2, 32, LN)]
+    scratch += [full, full, v(2 * PSYS, LN), full, full, full, v(2, NR, LN), v(2 * KSYS, LN), full, full, full, v(2, 32, LN)]
     scratch += [v(2, NR, LN), v(2, 32, LN), v(2, 32, LN)] * 2
     scratch += [v(2, 32, LN)] * 8
     scratch += [v(2, NR, LN), v(2, 32, LN), v(2, 32, LN), v(2, NR, LN), v(2, 32, LN)]
     scratch += [v(2, 2, NR, LN), v(2, 2, 32, LN), v(2, 2, 32, LN)]
     scratch += [v(2, 2, 8, 1, LN), v(2, 8, LN), v(2, 8, LN), v(8, LN)]
-    scratch += [sem(6, 2), sem(2, 6), sem(2, 6), sem(2, 3), sem(2, 3), sem(2, 3), sem(2, 2, 3), sem(2, 2, 8), sem(2, 2, 8), sem(2)]
+    scratch += [sem(6, 2), sem(2, 6), sem(2, 6), sem(2, 3), sem(2, 3), sem(2, 3), sem(2, 2, 3), sem(2, 2, 8), sem(2, 2, 8)]
     xp, hist = pl.pallas_call(
         kernel,
-        out_shape=(jax.ShapeDtypeStruct((2 * SYS, LN), F32), jax.ShapeDtypeStruct((8, LN), F32)),
+        out_shape=(pltpu.VMEM((2 * SYS, LN), F32), pltpu.VMEM((8, LN), F32)),
         in_specs=[pl.BlockSpec(memory_space=pl.ANY)] * 6,
-        out_specs=(pl.BlockSpec(memory_space=pl.ANY), pl.BlockSpec(memory_space=pltpu.VMEM)),
+        out_specs=(pl.BlockSpec(memory_space=pltpu.VMEM), pl.BlockSpec(memory_space=pltpu.VMEM)),
         scratch_shapes=scratch,
         compiler_params=pltpu.CompilerParams(collective_id=0, has_side_effects=True, vmem_limit_bytes=VMEM_MAIN),
         name='cg',
@@ -499,10 +481,10 @@
     return pl.pallas_call(
         unpack,
         out_shape=(jax.ShapeDtypeStruct((2, 64, 64, 64), F32), jax.ShapeDtypeStruct((2, ITERS + 1), F32)),
-        in_specs=[pl.BlockSpec(memory_space=pl.ANY)] * 2,
+        in_specs=[pl.BlockSpec(memory_space=pltpu.VMEM)] * 2,
         out_specs=[pl.BlockSpec(memory_space=pl.ANY)] * 2,
-        scratch_shapes=[v(2 * SYS, LN), v(2, 64, 64, 64), v(8, LN), v(2, ITERS + 1), sem(2 * CHUNKS), sem(2 * CHUNKS, 2), sem(2)],
-        compiler_params=pltpu.CompilerParams(vmem_limit_bytes=60 * 1024 * 1024),
+        scratch_shapes=[v(2, 64, 64, 64), v(2, ITERS + 1), sem(2 * CHUNKS, 2), pltpu.SemaphoreType.DMA],
+        compiler_params=pltpu.CompilerParams(vmem_limit_bytes=12 * 1024 * 1024),
         name='unpack',
     )(xp, hist)
 

time: 172 us -> 171 us (level)
  no operation moved by 1% of the time
where the time goes in v12:
time: 171 us
  Pallas kernels  170 us (99%)
    pallas_call x1, Pallas kernels, run(): pl.pallas_call(kernel, out_shape=(pltpu.VMEM((2 * SYS, LN), F32), pltpu.V...  168 us

profile of v12, /device:TPU:0, one launch (start us, length us, event | category | flops | bytes accessed | tf_op | source)
XLA Modules:
  0.0 171.1 jit_solution(14844865689844327083)
XLA Ops:
  0.6 168.2 %cg.1 = (f32[4096,128]{1,0:T(8,128)S(1)}, f32[8,128]{1,0:T(8,128)S(1)}) custom-call(f32[2,64,64,64]{3,2,1,0:T(8,128)} %s_hbm.1, f32[2,64,64,64]{3,2,1,0:T(8,128)} %b_hbm.1, f32[2,64,64,64]{3,2,1,0:T(8,128)} %x0_hbm.1, f32[2,64,64,64]{3,2,1,0:T(8,128)} %kx_hbm.1, f32[2,64,64,64]{3,2,1,0:T(8,128)} %ky_hbm.1, f32[2,64,64,64]{3,2,1,0:T(8,128)} %kz_hbm.1), custom_call_target="tpu_custom_call" | custom-call | tf_op jit(solution)/shard_map/cg/pallas_call | solution.py:472
  168.8 2.3 %unpack.1 = (f32[2,64,64,64]{3,2,1,0:T(8,128)}, f32[2,21]{1,0:T(2,128)}) custom-call(f32[4096,128]{1,0:T(8,128)S(1)} %get-tuple-element.4.buf, f32[8,128]{1,0:T(8,128)S(1)} %get-tuple-element.5.hist), custom_call_target="tpu_custom_call" | custom-call | tf_op jit(solution)/shard_map/unpack/pallas_call | solution.py:481

commit v13 on v12

--- a/solution.py
+++ b/solution.py
@@ -214,7 +214,7 @@
     def z_face(ref, c, to_sz, to_sy):
         def plane(x, T):
             return pick(T, ref[rows(x, c)], x, zf)
-        to_sz[c] = lax.fori_loop(0, NP, plane, zero32, unroll=8)
+        to_sz[c] = lax.fori_loop(0, NP, plane, zero32, unroll=16)
         to_sy[c] = ref[pl.ds(c * SYS + yf, 32, stride=NR)]
 
     def turn_r(c):
@@ -224,7 +224,7 @@
         def plane(x, carry):
             RZ[rows(x, c)] = jnp.where(mask, spread(G, x, zf), roll(R[rows(x, c)], to_z))
             return carry
-        lax.fori_loop(0, NP, plane, 0, unroll=8)
+        lax.fori_loop(0, NP, plane, 0, unroll=16)
 
     def r_copies(c):
         return [
@@ -278,9 +278,9 @@
         for cp in r_copies(c):
             cp.start()
 
-    start(0)
     prepare_kx(1)
     first[1][5].start()
+    start(0)
     prepare_sb(1)
     start(1)
     hist_s[...] = jnp.zeros((8, LN), F32)

time: 171 us -> 170 us (level)
  no operation moved by 1% of the time
where the time goes in v13:
time: 170 us
  Pallas kernels  170 us (100%)
    pallas_call x1, Pallas kernels, run(): pl.pallas_call(kernel, out_shape=(pltpu.VMEM((2 * SYS, LN), F32), pltpu.V...  167 us

profile of v13, /device:TPU:0, one launch (start us, length us, event | category | flops | bytes accessed | tf_op | source)
XLA Modules:
  0.0 170.3 jit_solution(2454676269165371832)
XLA Ops:
  0.6 167.4 %cg.1 = (f32[4096,128]{1,0:T(8,128)S(1)}, f32[8,128]{1,0:T(8,128)S(1)}) custom-call(f32[2,64,64,64]{3,2,1,0:T(8,128)} %s_hbm.1, f32[2,64,64,64]{3,2,1,0:T(8,128)} %b_hbm.1, f32[2,64,64,64]{3,2,1,0:T(8,128)} %x0_hbm.1, f32[2,64,64,64]{3,2,1,0:T(8,128)} %kx_hbm.1, f32[2,64,64,64]{3,2,1,0:T(8,128)} %ky_hbm.1, f32[2,64,64,64]{3,2,1,0:T(8,128)} %kz_hbm.1), custom_call_target="tpu_custom_call" | custom-call | tf_op jit(solution)/shard_map/cg/pallas_call | solution.py:472
  168.0 2.3 %unpack.1 = (f32[2,64,64,64]{3,2,1,0:T(8,128)}, f32[2,21]{1,0:T(2,128)}) custom-call(f32[4096,128]{1,0:T(8,128)S(1)} %get-tuple-element.4.buf, f32[8,128]{1,0:T(8,128)S(1)} %get-tuple-element.5.hist), custom_call_target="tpu_custom_call" | custom-call | tf_op jit(solution)/shard_map/unpack/pallas_call | solution.py:481

commit v14 on v13

--- a/solution.py
+++ b/solution.py
@@ -17,7 +17,7 @@
 SYS = NP * NR
 PSYS = (NP + 1) * PR
 KSYS = NP * KR
-IN_FLIGHT = 3
+IN_FLIGHT = 5
 AHEAD = 3
 
 
@@ -214,7 +214,7 @@
     def z_face(ref, c, to_sz, to_sy):
         def plane(x, T):
             return pick(T, ref[rows(x, c)], x, zf)
-        to_sz[c] = lax.fori_loop(0, NP, plane, zero32, unroll=16)
+        to_sz[c] = lax.fori_loop(0, NP, plane, zero32, unroll=32)
         to_sy[c] = ref[pl.ds(c * SYS + yf, 32, stride=NR)]
 
     def turn_r(c):
@@ -224,7 +224,7 @@
         def plane(x, carry):
             RZ[rows(x, c)] = jnp.where(mask, spread(G, x, zf), roll(R[rows(x, c)], to_z))
             return carry
-        lax.fori_loop(0, NP, plane, 0, unroll=16)
+        lax.fori_loop(0, NP, plane, 0, unroll=32)
 
     def r_copies(c):
         return [

time: 170 us -> 170 us (level)
  no operation moved by 1% of the time
where the time goes in v14:
time: 170 us
  Pallas kernels  169 us (99%)
    pallas_call x1, Pallas kernels, run(): pl.pallas_call(kernel, out_shape=(pltpu.VMEM((2 * SYS, LN), F32), pltpu.V...  167 us

profile of v14, /device:TPU:0, one launch (start us, length us, event | category | flops | bytes accessed | tf_op | source)
XLA Modules:
  0.0 169.7 jit_solution(8545631985775160607)
XLA Ops:
  0.6 166.7 %cg.1 = (f32[4096,128]{1,0:T(8,128)S(1)}, f32[8,128]{1,0:T(8,128)S(1)}) custom-call(f32[2,64,64,64]{3,2,1,0:T(8,128)} %s_hbm.1, f32[2,64,64,64]{3,2,1,0:T(8,128)} %b_hbm.1, f32[2,64,64,64]{3,2,1,0:T(8,128)} %x0_hbm.1, f32[2,64,64,64]{3,2,1,0:T(8,128)} %kx_hbm.1, f32[2,64,64,64]{3,2,1,0:T(8,128)} %ky_hbm.1, f32[2,64,64,64]{3,2,1,0:T(8,128)} %kz_hbm.1), custom_call_target="tpu_custom_call" | custom-call | tf_op jit(solution)/shard_map/cg/pallas_call | solution.py:472
  167.4 2.3 %unpack.1 = (f32[2,64,64,64]{3,2,1,0:T(8,128)}, f32[2,21]{1,0:T(2,128)}) custom-call(f32[4096,128]{1,0:T(8,128)S(1)} %get-tuple-element.4.buf, f32[8,128]{1,0:T(8,128)S(1)} %get-tuple-element.5.hist), custom_call_target="tpu_custom_call" | custom-call | tf_op jit(solution)/shard_map/unpack/pallas_call | solution.py:481

commit v15 on v14

--- a/solution.py
+++ b/solution.py
@@ -118,7 +118,7 @@
             PB[pl.ds(base + 72, 8)] = jnp.zeros((8, LN), F32)
             PB[pl.ds(base + 8, NR)] = u
             return pick(T, u, x, zf)
-        sxz[c] = lax.fori_loop(0, NP, pack_x, zero32, unroll=8)
+        sxz[c] = lax.fori_loop(0, NP, pack_x, zero32, unroll=16)
         sxy[c] = X[pl.ds(c * SYS + yf, 32, stride=NR)]
 
     def prepare_kz(c):
@@ -131,7 +131,7 @@
             KZ[rows(x, c)] = jnp.where(pz == 1, moved, inner)
             KZF[rows(x, c)] = jnp.where(pz == 1, inner, moved)
             return pick(T, u, x, 63)
-        skz[c] = lax.fori_loop(0, NP, pack_z, zero32, unroll=8)
+        skz[c] = lax.fori_loop(0, NP, pack_z, zero32, unroll=16)
 
     def prepare_ky(c):
         loaded(2, c)
@@ -142,7 +142,7 @@
             u = jnp.where(jnp.logical_and(row == NR - 1, py == 1), 0.0, u)
             KY[pl.ds(pl.multiple_of(c * KSYS + x * KR + 8, 8), NR)] = u
             return carry
-        lax.fori_loop(0, NP, pack_ky, 0, unroll=8)
+        lax.fori_loop(0, NP, pack_ky, 0, unroll=16)
         sky[c] = KY[pl.ds(c * KSYS + 71, 32, stride=KR)]
 
     def prepare_kx(c):
@@ -151,7 +151,7 @@
         def pack_kx(x, carry):
             KX[rows(x, c)] = packed(st_kx, c, x)
             return carry
-        lax.fori_loop(0, NP, pack_kx, 0, unroll=8)
+        lax.fori_loop(0, NP, pack_kx, 0, unroll=16)
         last = KX[pl.ds(c * SYS + 31 * NR, NR)]
         edge = jnp.logical_and(lanes(NR) >= 64, px == 1)
         KX[pl.ds(c * SYS + 31 * NR, NR)] = jnp.where(edge, 0.0, last)
@@ -164,7 +164,7 @@
             D[rows(x, c)] = packed(st_s, c, x)
             R[rows(x, c)] = packed(st_b, c, x)
             return carry
-        lax.fori_loop(0, NP, pack_sb, 0, unroll=8)
+        lax.fori_loop(0, NP, pack_sb, 0, unroll=16)
 
     prepare_x0(0)
     pl.semaphore_wait(barrier, 7)

time: 170 us -> 171 us (level)
  no operation moved by 1% of the time
where the time goes in v15:
time: 171 us
  Pallas kernels  170 us (99%)
    pallas_call x1, Pallas kernels, run(): pl.pallas_call(kernel, out_shape=(pltpu.VMEM((2 * SYS, LN), F32), pltpu.V...  168 us

profile of v15, /device:TPU:0, one launch (start us, length us, event | category | flops | bytes accessed | tf_op | source)
XLA Modules:
  0.0 171.1 jit_solution(15418407360961439379)
XLA Ops:
  0.6 168.2 %cg.1 = (f32[4096,128]{1,0:T(8,128)S(1)}, f32[8,128]{1,0:T(8,128)S(1)}) custom-call(f32[2,64,64,64]{3,2,1,0:T(8,128)} %s_hbm.1, f32[2,64,64,64]{3,2,1,0:T(8,128)} %b_hbm.1, f32[2,64,64,64]{3,2,1,0:T(8,128)} %x0_hbm.1, f32[2,64,64,64]{3,2,1,0:T(8,128)} %kx_hbm.1, f32[2,64,64,64]{3,2,1,0:T(8,128)} %ky_hbm.1, f32[2,64,64,64]{3,2,1,0:T(8,128)} %kz_hbm.1), custom_call_target="tpu_custom_call" | custom-call | tf_op jit(solution)/shard_map/cg/pallas_call | solution.py:472
  168.8 2.3 %unpack.1 = (f32[2,64,64,64]{3,2,1,0:T(8,128)}, f32[2,21]{1,0:T(2,128)}) custom-call(f32[4096,128]{1,0:T(8,128)S(1)} %get-tuple-element.4.buf, f32[8,128]{1,0:T(8,128)S(1)} %get-tuple-element.5.hist), custom_call_target="tpu_custom_call" | custom-call | tf_op jit(solution)/shard_map/unpack/pallas_call | solution.py:481

commit v16 on v14

--- a/solution.py
+++ b/solution.py
@@ -17,7 +17,7 @@
 SYS = NP * NR
 PSYS = (NP + 1) * PR
 KSYS = NP * KR
-IN_FLIGHT = 5
+IN_FLIGHT = 7
 AHEAD = 3
 
 
@@ -391,7 +391,7 @@
         def step_x(x, carry):
             X[rows(x, c)] = X[rows(x, c)] + a_pl * PB[pl.ds(pl.multiple_of(c * PSYS + x * PR + 8, 8), NR)]
             return carry
-        lax.fori_loop(0, NP, step_x, 0, unroll=4)
+        lax.fori_loop(0, NP, step_x, 0, unroll=8)
         reduce_sent(1, c)
 
     def body(k, carry):

time: 170 us -> 170 us (level)
  no operation moved by 1% of the time
where the time goes in v16:
time: 170 us
  Pallas kernels  169 us (99%)
    pallas_call x1, Pallas kernels, run(): pl.pallas_call(kernel, out_shape=(pltpu.VMEM((2 * SYS, LN), F32), pltpu.V...  167 us

profile of v16, /device:TPU:0, one launch (start us, length us, event | category | flops | bytes accessed | tf_op | source)
XLA Modules:
  0.0 169.7 jit_solution(3236350790920334925)
XLA Ops:
  0.6 166.7 %cg.1 = (f32[4096,128]{1,0:T(8,128)S(1)}, f32[8,128]{1,0:T(8,128)S(1)}) custom-call(f32[2,64,64,64]{3,2,1,0:T(8,128)} %s_hbm.1, f32[2,64,64,64]{3,2,1,0:T(8,128)} %b_hbm.1, f32[2,64,64,64]{3,2,1,0:T(8,128)} %x0_hbm.1, f32[2,64,64,64]{3,2,1,0:T(8,128)} %kx_hbm.1, f32[2,64,64,64]{3,2,1,0:T(8,128)} %ky_hbm.1, f32[2,64,64,64]{3,2,1,0:T(8,128)} %kz_hbm.1), custom_call_target="tpu_custom_call" | custom-call | tf_op jit(solution)/shard_map/cg/pallas_call | solution.py:472
  167.4 2.3 %unpack.1 = (f32[2,64,64,64]{3,2,1,0:T(8,128)}, f32[2,21]{1,0:T(2,128)}) custom-call(f32[4096,128]{1,0:T(8,128)S(1)} %get-tuple-element.4.buf, f32[8,128]{1,0:T(8,128)S(1)} %get-tuple-element.5.hist), custom_call_target="tpu_custom_call" | custom-call | tf_op jit(solution)/shard_map/unpack/pallas_call | solution.py:481

commit v17 on v16

--- a/solution.py
+++ b/solution.py
@@ -249,7 +249,7 @@
         mask = face_mask(NR)
 
         def start_plane(x, carry):
-            acc, fx_prev, kx_prev, u = carry
+            acc, fx_prev, kx_prev, u, T = carry
             base = pl.multiple_of(c * PSYS + x * PR, 8)
             at = rows(x, c)
             kbase = pl.multiple_of(c * KSYS + x * KR, 8)
@@ -270,11 +270,12 @@
             PZ[at] = uz
             r = R[at] - (s * u + (fx - fx_prev) + (kyv * (u - yu) - kyl * (yl - u)) + (fz - fz_away))
             R[at] = r
-            return acc + fold(r * r), fx, kxv, nxt
-        init = (jnp.zeros((8, LN), F32), KXM[c] * (low - u_first), KXM[c], u_first)
-        acc = lax.fori_loop(0, NP, start_plane, init, unroll=4)[0]
+            return acc + fold(r * r), fx, kxv, nxt, pick(T, r, x, zf)
+        init = (jnp.zeros((8, LN), F32), KXM[c] * (low - u_first), KXM[c], u_first, zero32)
+        acc, _, _, _, T = lax.fori_loop(0, NP, start_plane, init, unroll=4)
         reduce_start(0, c, acc)
-        z_face(R, c, srz, sry)
+        srz[c] = T
+        sry[c] = R[pl.ds(c * SYS + yf, 32, stride=NR)]
         for cp in r_copies(c):
             cp.start()
 

time: 170 us -> 170 us (level)
  no operation moved by 1% of the time
where the time goes in v17:
time: 170 us
  Pallas kernels  169 us (99%)
    pallas_call x1, Pallas kernels, run(): pl.pallas_call(kernel, out_shape=(pltpu.VMEM((2 * SYS, LN), F32), pltpu.V...  167 us

profile of v17, /device:TPU:0, one launch (start us, length us, event | category | flops | bytes accessed | tf_op | source)
XLA Modules:
  0.0 170.0 jit_solution(17614516355080625701)
XLA Ops:
  0.6 167.1 %cg.1 = (f32[4096,128]{1,0:T(8,128)S(1)}, f32[8,128]{1,0:T(8,128)S(1)}) custom-call(f32[2,64,64,64]{3,2,1,0:T(8,128)} %s_hbm.1, f32[2,64,64,64]{3,2,1,0:T(8,128)} %b_hbm.1, f32[2,64,64,64]{3,2,1,0:T(8,128)} %x0_hbm.1, f32[2,64,64,64]{3,2,1,0:T(8,128)} %kx_hbm.1, f32[2,64,64,64]{3,2,1,0:T(8,128)} %ky_hbm.1, f32[2,64,64,64]{3,2,1,0:T(8,128)} %kz_hbm.1), custom_call_target="tpu_custom_call" | custom-call | tf_op jit(solution)/shard_map/cg/pallas_call | solution.py:473
  167.7 2.3 %unpack.1 = (f32[2,64,64,64]{3,2,1,0:T(8,128)}, f32[2,21]{1,0:T(2,128)}) custom-call(f32[4096,128]{1,0:T(8,128)S(1)} %get-tuple-element.4.buf, f32[8,128]{1,0:T(8,128)S(1)} %get-tuple-element.5.hist), custom_call_target="tpu_custom_call" | custom-call | tf_op jit(solution)/shard_map/unpack/pallas_call | solution.py:482
